TPU v7x, 32 devices: a 4x2x2 block of a 4x4x8 slice. The times are simulated.
32 devices in a mesh: dp: 4 (over y, z), tp: 8 (over x, core).
Axes of the slice: x: 4, y: 2, z: 2, core: 2. Of those that a mesh axis runs over, the one named last changes fastest.
The devices are a block of a 4x4x8 slice.
Arguments:
- tokens: bfloat16 [8, 512, 4672], P('dp', 'tp'), parts along dimension 0
- pad_mask: int32 [8, 512], P('dp'), parts along dimension 0
- rel_table: float32 [32, 64], P(None, 'tp')
- w_query: bfloat16 [2, 4672, 4096], P(None, None, 'tp')
- w_key: bfloat16 [2, 4672, 4096], P(None, None, 'tp')
- w_value: bfloat16 [2, 4672, 4096], P(None, None, 'tp')
- w_out: bfloat16 [2, 4096, 4672], P(None, 'tp')
- w_act: bfloat16 [2, 4672, 12352], P(None, None, 'tp')
- w_lin: bfloat16 [2, 4672, 12352], P(None, None, 'tp')
- w_down: bfloat16 [2, 12352, 4672], P(None, 'tp')
- norm_attn: float32 [2, 4672], replicated
- norm_mlp: float32 [2, 4672], replicated
Outputs:
- output: bfloat16 [8, 512, 4672], P('dp', 'tp'), parts along dimension 0
There are 4 independent parts. A program takes and returns all parts, laid end to end along the dimension named above; an argument that names none is the same for every part.
All inputs are finite; a program needn't handle non-finite values.
Results may differ from a plain program's by a relative error of at most 0.02.
Values are sent between devices in bfloat16 or wider.
A program may use at most 768 MiB of HBM per device.

v0:
```python
import jax
import jax.numpy as jnp
from jax import lax
from jax.sharding import PartitionSpec as P


def rel_bucket(offsets):
    side = jnp.where(offsets > 0, 16, 0)
    distance = jnp.minimum(jnp.abs(offsets), 128)
    limits = 64 * 2 ** jnp.arange(1, 8)
    steps = jnp.sum((distance[:, None] * distance[:, None] >= limits[None, :]).astype(jnp.int32), axis=1)
    return side + jnp.where(distance < 8, distance, 8 + steps)


def rms_norm(rows_in, gain_vec):
    rows32 = rows_in.astype(jnp.float32)
    inv_rms = lax.rsqrt(jnp.mean(rows32 * rows32, axis=-1, keepdims=True) + 1e-6)
    return (rows32 * inv_rms * gain_vec).astype(jnp.bfloat16)


def bias_rows(dist_table, seq_len, row_start, row_count):
    padded = jnp.pad(dist_table, ((0, 0), (0, 1)))
    doubled = jnp.concatenate([padded, padded], axis=1)
    shifted = lax.dynamic_slice_in_dim(doubled, 2 * seq_len - row_start, 2 * seq_len, axis=1)
    tiled = jnp.tile(shifted, (1, row_count))[:, : row_count * (2 * seq_len - 1)]
    return tiled.reshape(dist_table.shape[0], row_count, 2 * seq_len - 1)[:, :, seq_len - 1:]


def solution(mesh):
    group_size = mesh.shape['tp']
    col_spec = P(None, None, 'tp')
    row_spec = P(None, 'tp', None)

    def local_fn(tokens, pad_mask, rel_table, w_query, w_key, w_value, w_out, w_act, w_lin, w_down, norm_attn, norm_mlp):
        batch, seq_loc, model_dim = tokens.shape
        seq_len = seq_loc * group_size
        head_count = rel_table.shape[1]
        head_dim = w_query.shape[2] // head_count
        offsets = jnp.arange(2 * seq_len - 1) - (seq_len - 1)
        rel_bias = bias_rows(jnp.take(rel_table.T, rel_bucket(offsets), axis=1), seq_len, 0, seq_len)
        key_bias = jnp.where(pad_mask == 1, 0.0, -1e9).astype(jnp.float32)[:, None, None, :]

        def project(gathered, weight_mat):
            projected = jnp.einsum('bsd,dn->bsn', gathered, weight_mat, preferred_element_type=jnp.float32)
            return projected.astype(jnp.bfloat16).reshape(batch, seq_len, head_count, head_dim)

        residual = tokens
        for layer_idx in range(w_query.shape[0]):
            gathered = lax.all_gather(rms_norm(residual, norm_attn[layer_idx]), 'tp', axis=1, tiled=True)
            query_proj = project(gathered, w_query[layer_idx])
            key_proj = project(gathered, w_key[layer_idx])
            value_proj = project(gathered, w_value[layer_idx])
            scores = jnp.einsum('bqhe,bkhe->bhqk', query_proj, key_proj, preferred_element_type=jnp.float32)
            attn_probs = jax.nn.softmax(scores + rel_bias + key_bias, axis=-1).astype(jnp.bfloat16)
            context = jnp.einsum('bhqk,bkhe->bqhe', attn_probs, value_proj, preferred_element_type=jnp.float32).astype(jnp.bfloat16)
            out_mat = w_out[layer_idx].reshape(head_count, head_dim, model_dim)
            part_out = jnp.einsum('crif,ife->cre', context, out_mat, preferred_element_type=jnp.float32).astype(jnp.bfloat16)
            attn_out = lax.psum_scatter(part_out, 'tp', scatter_dimension=1, tiled=True)
            mid_resid = (residual.astype(jnp.float32) + attn_out.astype(jnp.float32)).astype(jnp.bfloat16)
            gathered = lax.all_gather(rms_norm(mid_resid, norm_mlp[layer_idx]), 'tp', axis=1, tiled=True)
            act_proj = jnp.einsum('bsd,df->bsf', gathered, w_act[layer_idx], preferred_element_type=jnp.float32)
            lin_proj = jnp.einsum('bsd,df->bsf', gathered, w_lin[layer_idx], preferred_element_type=jnp.float32)
            gated = (jax.nn.gelu(act_proj, approximate=True) * lin_proj).astype(jnp.bfloat16)
            part_out = jnp.einsum('bsf,fd->bsd', gated, w_down[layer_idx], preferred_element_type=jnp.float32).astype(jnp.bfloat16)
            ffn_out = lax.psum_scatter(part_out, 'tp', scatter_dimension=1, tiled=True)
            residual = (mid_resid.astype(jnp.float32) + ffn_out.astype(jnp.float32)).astype(jnp.bfloat16)
        return residual

    in_specs = (P('dp', 'tp', None), P('dp', None), P(None, 'tp'), col_spec, col_spec, col_spec, row_spec,
                col_spec, col_spec, row_spec, P(None, None), P(None, None))
    return jax.shard_map(local_fn, mesh=mesh, in_specs=in_specs, out_specs=P('dp', 'tp', None), check_vma=False)
```

profile of v0, /device:TPU:81, one launch (start us, length us, event | category | flops | bytes accessed | tf_op | source)
XLA Modules:
  0.0 741.1 jit_solution(1522484437283801320)
XLA Ops:
  6.6 1.5 slice_reduce_fusion.1
  8.1 1.6 fusion.74
  9.7 2.7 fusion.76
  12.4 0.1 all-gather.5.cloned.1.call-update
  12.4 0.1 reduce-scatter.5.cloned.1.call-start
  12.5 0.8 copy.22
  13.3 0.1 convert_reduce_fusion
  13.4 2.8 gather_fusion
  16.3 0.2 select_bitcast_fusion
  16.5 0.2 copy.33
  16.7 2.1 tile.4
  18.8 6.0 slice.82
  24.8 12.6 %reshape.190 = f32[4190208]{0:T(1024)} reshape(f32[8,523776]{1,0:T(8,128)} %slice.82) | data formatting | bytes 33521664
  37.4 17.2 %reshape.158 = f32[8,512,1023]{2,1,0:T(8,128)} reshape(f32[4190208]{0:T(1024)} %reshape.190) | data formatting | bytes 33521664 | tf_op jit(solution)/shard_map/reshape | solution.py:26
  54.6 9.4 %slice.83 = f32[8,512,512]{2,1,0:T(8,128)} slice(f32[8,512,1023]{2,1,0:T(8,128)} %reshape.158), slice={[0:8], [0:512], [511:1023]} | slice | bytes 16777216 | tf_op jit(solution)/shard_map/slice | solution.py:26
  64.0 9.1 %copy.24 = f32[8,512,512]{1,2,0:T(8,128)} copy(f32[8,512,512]{2,1,0:T(8,128)} %slice.83) | data formatting | bytes 16777216 | tf_op jit(solution)/shard_map/slice | solution.py:26
  73.1 8.1 %fusion.122 = (bf16[1,512,4672]{1,2,0:T(8,128)(2,1)}, bf16[1,512,4672]{1,2,0:T(8,128)(2,1)}) fusion(bf16[2,512,4672]{1,2,0:T(8,128)(2,1)} %param.18), kind=kLoop, calls=%fused_computation.149 | loop fusion | bytes 19136512 | tf_op jit(solution)/shard_map/slice | solution.py:56
  81.3 7.3 copy.26
  88.6 9.6 %fusion.99 = bf16[2,512,512]{1,2,0:T(8,128)(2,1)S(1)} fusion(bf16[2,512,4672]{2,1,0:T(8,128)(2,1)} %all-gather.5.cloned.1.call-done, bf16[2,4672,512]{2,1,0:T(8,128)(2,1)} %param.15), kind=kOutput, calls=%fused_computation.110 | convolution fusion | flops 4899471360 | bytes 15532032 | tf_op jit(solution)/shard_map/bsd,dn->bsn/dot_general | solution.py:44
  98.2 7.6 %fusion.102 = bf16[2,512,512]{1,2,0:T(8,128)(2,1)S(1)} fusion(bf16[2,512,4672]{2,1,0:T(8,128)(2,1)S(1)} %copy-done.8, bf16[2,4672,512]{2,1,0:T(8,128)(2,1)} %param.16), kind=kOutput, calls=%fused_computation.111 | convolution fusion | flops 4899471360 | bytes 15400960 | tf_op jit(solution)/shard_map/bsd,dn->bsn/dot_general | solution.py:44
  105.8 11.7 %fusion.123 = (f32[2,8,512]{2,1,0:T(8,128)S(1)}, f32[2,8,512,512]{2,3,1,0:T(8,128)}) fusion(f32[2,512]{1,0:T(2,128)S(1)} %compare_select_fusion.5, f32[8,512,512]{1,2,0:T(8,128)} %copy.24, bf16[2,512,8,64]{1,3,2,0:T(8,128)(2,1)S(1)} %bitcast.130, bf16[2,512,8,64]{1,3,2,0:T(8,128)(2,1)S(1)} %bitcast.131), kind=kOutput, calls=%fused_computation.150 | convolution fusion | flops 553648640 | bytes 27299840 | tf_op jit(solution)/shard_map/sub | solution.py:54
  117.5 9.5 %fusion.96 = bf16[2,512,512]{1,2,0:T(8,128)(2,1)S(1)} fusion(bf16[2,512,4672]{2,1,0:T(8,128)(2,1)} %all-gather.5.cloned.1.call-done, bf16[2,4672,512]{2,1,0:T(8,128)(2,1)} %param.17), kind=kOutput, calls=%fused_computation.109 | convolution fusion | flops 4899471360 | bytes 15532032 | tf_op jit(solution)/shard_map/bsd,dn->bsn/dot_general | solution.py:44
  126.9 14.2 %bitcast_convert_fusion.1 = bf16[2,512,4672]{2,1,0:T(8,128)(2,1)} fusion(bf16[8,64,4672,1]{2,1,0,3:T(8,128)(2,1)} %bitcast.126, bf16[2,512,8,64]{1,3,2,0:T(8,128)(2,1)S(1)} %bitcast.134, f32[2,8,512,512]{2,3,1,0:T(8,128)} %get-tuple-element.14, f32[2,8,512]{2,1,0:T(8,128)S(1)} %get-tuple-element.13), kind=kOutput, calls=%fused_computation.4 | convolution fusion | flops 5449515008 | bytes 32210944 | tf_op jit(solution)/shard_map/crif,ife->cre/dot_general | solution.py:57
  141.1 0.1 reduce-scatter.5.cloned.1.call-update
  141.2 0.5 all-gather.7.cloned.1.call-start
  141.6 0.2 copy-done.6
  141.9 0.7 slice_reduce_fusion.2
  142.6 58.1 %reduce-scatter.5.cloned.1.call-done = bf16[2,64,4672]{2,1,0:T(8,128)(2,1)} async-done(((bf16[2,512,4672]{2,1,0:T(8,128)(2,1)}), bf16[2,64,4672]{2,1,0:T(8,128)(2,1)}) %reduce-scatter.5.cloned.1.call-update) | async-done | bytes 1196048 | tf_op jit(solution)/shard_map/reduce_scatter | solution.py:58
  200.7 1.8 fusion.78
  202.4 2.7 fusion.80
  205.2 0.1 all-gather.7.cloned.1.call-update
  205.2 0.1 reduce-scatter.7.cloned.1.call-start
  205.3 52.6 %all-gather.7.cloned.1.call-done = bf16[2,512,4672]{2,1,0:T(8,128)(2,1)} async-done(((bf16[2,64,4672]{2,1,0:T(8,128)(2,1)}), bf16[2,512,4672]{2,1,0:T(8,128)(2,1)}) %all-gather.7.cloned.1.call-update) | async-done | bytes 9568272 | tf_op jit(solution)/shard_map/all_gather | solution.py:60
  257.9 24.0 %fusion.10 = f32[2,512,1544]{1,2,0:T(8,128)} fusion(bf16[2,512,4672]{2,1,0:T(8,128)(2,1)} %all-gather.7.cloned.1.call-done, bf16[2,4672,1544]{1,2,0:T(8,128)(2,1)} %param.20), kind=kOutput, calls=%fused_computation.19 | convolution fusion | flops 14773387264 | bytes 30648320 | tf_op jit(solution)/shard_map/bsd,df->bsf/dot_general | solution.py:62
  281.9 21.9 %fusion.42 = bf16[2,512,1544]{1,2,0:T(8,128)(2,1)} fusion(f32[2,512,1544]{1,2,0:T(8,128)} %fusion.10, bf16[2,512,4672]{2,1,0:T(8,128)(2,1)S(1)} %copy-done.10, bf16[2,4672,1544]{1,2,0:T(8,128)(2,1)} %param.19), kind=kOutput, calls=%fused_computation.49 | convolution fusion | flops 14789197824 | bytes 33679360 | tf_op jit(solution)/shard_map/bsd,df->bsf/dot_general | solution.py:61
  303.9 25.1 %fusion.22 = bf16[2,512,4672]{2,1,0:T(8,128)(2,1)} fusion(bf16[2,512,1544]{1,2,0:T(8,128)(2,1)} %fusion.42, bf16[2,1544,4672]{2,1,0:T(8,128)(2,1)} %param.21), kind=kOutput, calls=%fused_computation.33 | convolution fusion | flops 14778171392 | bytes 27355136 | tf_op jit(solution)/shard_map/bsf,fd->bsd/dot_general | solution.py:64
  329.0 0.1 reduce-scatter.7.cloned.1.call-update
  329.0 0.1 all-gather.9.cloned.1.call-start
  329.1 55.1 %reduce-scatter.7.cloned.1.call-done = bf16[2,64,4672]{2,1,0:T(8,128)(2,1)} async-done(((bf16[2,512,4672]{2,1,0:T(8,128)(2,1)}), bf16[2,64,4672]{2,1,0:T(8,128)(2,1)}) %reduce-scatter.7.cloned.1.call-update) | async-done | bytes 1196048 | tf_op jit(solution)/shard_map/reduce_scatter | solution.py:65
  384.2 2.3 fusion.82
  386.6 1.4 fusion.84
  388.0 0.1 all-gather.9.cloned.1.call-update
  388.0 0.1 reduce-scatter.9.cloned.1.call-start
  388.1 7.4 %copy.28 = bf16[1,512,4672]{2,1,0:T(8,128)(2,1)} copy(bf16[1,512,4672]{1,2,0:T(8,128)(2,1)} %get-tuple-element.12) | data formatting | bytes 9568256 | tf_op jit(solution)/shard_map/slice | solution.py:56
  395.5 45.2 %all-gather.9.cloned.1.call-done = bf16[2,512,4672]{2,1,0:T(8,128)(2,1)} async-done(((bf16[2,64,4672]{2,1,0:T(8,128)(2,1)}), bf16[2,512,4672]{2,1,0:T(8,128)(2,1)}) %all-gather.9.cloned.1.call-update) | async-done | bytes 9568272 | tf_op jit(solution)/shard_map/all_gather | solution.py:49
  440.7 9.6 %fusion.108 = bf16[2,512,512]{1,2,0:T(8,128)(2,1)S(1)} fusion(bf16[2,512,4672]{2,1,0:T(8,128)(2,1)} %all-gather.9.cloned.1.call-done, bf16[2,4672,512]{2,1,0:T(8,128)(2,1)} %param.15), kind=kOutput, calls=%fused_computation.113 | convolution fusion | flops 4899471360 | bytes 15532032 | tf_op jit(solution)/shard_map/bsd,dn->bsn/dot_general | solution.py:44
  450.3 7.4 fusion.111
  457.7 11.7 %fusion.124 = (f32[2,8,512]{2,1,0:T(8,128)S(1)}, f32[2,8,512,512]{2,3,1,0:T(8,128)}) fusion(f32[2,512]{1,0:T(2,128)S(1)} %copy-done.3, f32[8,512,512]{1,2,0:T(8,128)} %copy.24, bf16[2,512,8,64]{1,3,2,0:T(8,128)(2,1)S(1)} %bitcast.128, bf16[2,512,8,64]{1,3,2,0:T(8,128)(2,1)S(1)} %bitcast.129), kind=kOutput, calls=%fused_computation.151 | convolution fusion | flops 553648640 | bytes 27299840 | tf_op jit(solution)/shard_map/sub | solution.py:54
  469.4 9.5 %fusion.105 = bf16[2,512,512]{1,2,0:T(8,128)(2,1)S(1)} fusion(bf16[2,512,4672]{2,1,0:T(8,128)(2,1)} %all-gather.9.cloned.1.call-done, bf16[2,4672,512]{2,1,0:T(8,128)(2,1)} %param.17), kind=kOutput, calls=%fused_computation.112 | convolution fusion | flops 4899471360 | bytes 15532032 | tf_op jit(solution)/shard_map/bsd,dn->bsn/dot_general | solution.py:44
  478.9 14.4 %bitcast_convert_fusion = bf16[2,512,4672]{2,1,0:T(8,128)(2,1)} fusion(bf16[8,64,4672,1]{2,1,0,3:T(8,128)(2,1)} %bitcast.125, bf16[2,512,8,64]{1,3,2,0:T(8,128)(2,1)S(1)} %bitcast.135, f32[2,8,512,512]{2,3,1,0:T(8,128)} %get-tuple-element.16, f32[2,8,512]{2,1,0:T(8,128)S(1)} %get-tuple-element.15), kind=kOutput, calls=%fused_computation.3 | convolution fusion | flops 5449515008 | bytes 32210944 | tf_op jit(solution)/shard_map/crif,ife->cre/dot_general | solution.py:57
  493.2 0.1 reduce-scatter.9.cloned.1.call-update
  493.3 0.1 all-gather.11.cloned.1.call-start
  493.4 55.1 %reduce-scatter.9.cloned.1.call-done = bf16[2,64,4672]{2,1,0:T(8,128)(2,1)} async-done(((bf16[2,512,4672]{2,1,0:T(8,128)(2,1)}), bf16[2,64,4672]{2,1,0:T(8,128)(2,1)}) %reduce-scatter.9.cloned.1.call-update) | async-done | bytes 1196048 | tf_op jit(solution)/shard_map/reduce_scatter | solution.py:58
  548.5 1.8 fusion.86
  550.3 2.7 fusion.88
  553.0 0.1 all-gather.11.cloned.1.call-update
  553.1 0.1 reduce-scatter.11.cloned.1.call-start
  553.2 52.6 %all-gather.11.cloned.1.call-done = bf16[2,512,4672]{2,1,0:T(8,128)(2,1)} async-done(((bf16[2,64,4672]{2,1,0:T(8,128)(2,1)}), bf16[2,512,4672]{2,1,0:T(8,128)(2,1)}) %all-gather.11.cloned.1.call-update) | async-done | bytes 9568272 | tf_op jit(solution)/shard_map/all_gather | solution.py:60
  605.7 24.3 %fusion.4 = f32[2,512,1544]{1,2,0:T(8,128)} fusion(bf16[2,512,4672]{2,1,0:T(8,128)(2,1)} %all-gather.11.cloned.1.call-done, bf16[2,4672,1544]{1,2,0:T(8,128)(2,1)} %param.20), kind=kOutput, calls=%fused_computation.13 | convolution fusion | flops 14773387264 | bytes 30648320 | tf_op jit(solution)/shard_map/bsd,df->bsf/dot_general | solution.py:62
  630.0 21.0 %fusion.51 = bf16[2,512,1544]{1,2,0:T(8,128)(2,1)S(1)} fusion(f32[2,512,1544]{1,2,0:T(8,128)} %fusion.4, bf16[2,512,4672]{2,1,0:T(8,128)(2,1)S(1)} %copy-done.11, bf16[2,4672,1544]{1,2,0:T(8,128)(2,1)} %param.19), kind=kOutput, calls=%fused_computation.58 | convolution fusion | flops 14789197824 | bytes 33679360 | tf_op jit(solution)/shard_map/bsd,df->bsf/dot_general | solution.py:61
  651.0 24.9 %fusion.25 = bf16[2,512,4672]{2,1,0:T(8,128)(2,1)} fusion(bf16[2,512,1544]{1,2,0:T(8,128)(2,1)S(1)} %fusion.51, bf16[2,1544,4672]{2,1,0:T(8,128)(2,1)} %param.21), kind=kOutput, calls=%fused_computation.34 | convolution fusion | flops 14778171392 | bytes 27355136 | tf_op jit(solution)/shard_map/bsf,fd->bsd/dot_general | solution.py:64
  675.8 0.1 reduce-scatter.11.cloned.1.call-update
  675.9 55.2 %reduce-scatter.11.cloned.1.call-done = bf16[2,64,4672]{2,1,0:T(8,128)(2,1)} async-done(((bf16[2,512,4672]{2,1,0:T(8,128)(2,1)}), bf16[2,64,4672]{2,1,0:T(8,128)(2,1)}) %reduce-scatter.11.cloned.1.call-update) | async-done | bytes 1196048 | tf_op jit(solution)/shard_map/reduce_scatter | solution.py:65
  731.1 2.7 fusion.89
  (37 shorter events, 0.2 us)
Async XLA Ops:
  6.5 82.0 %all-gather.5.cloned.1.call-start = ((), (), s32[]{:S(2)}) async-start(), calls=%async_computation.4 | async-start | bytes 10911744 | tf_op jit(solution)/shard_map/all_gather | solution.py:49
  12.4 188.2 %reduce-scatter.5.cloned.1.call-start = ((), (), s32[]{:S(2)}) async-start(), calls=%async_computation.5 | async-start | bytes 10911744 | tf_op jit(solution)/shard_map/reduce_scatter | solution.py:58
  81.3 7.3 copy-start.7
  88.5 17.2 %copy-start.2 = (f32[2,512]{1,0:T(2,128)}, f32[2,512]{1,0:T(2,128)S(1)}, u32[]{:S(2)}) copy-start(f32[2,512]{1,0:T(2,128)S(1)} %compare_select_fusion.5) | copy-start | bytes 12292
  88.6 9.6 %copy-start.8 = (bf16[2,512,4672]{2,1,0:T(8,128)(2,1)S(1)}, bf16[2,512,4672]{2,1,0:T(8,128)(2,1)}, u32[]{:S(2)}) copy-start(bf16[2,512,4672]{2,1,0:T(8,128)(2,1)} %all-gather.5.cloned.1.call-done) | copy-start | bytes 28704772
  141.1 0.8 copy-start.6
  141.1 59.6 %copy-start = (bf16[2,64,4672]{2,1,0:T(8,128)(2,1)S(1)}, bf16[2,64,4672]{2,1,0:T(8,128)(2,1)}, u32[]{:S(2)}) copy-start(bf16[2,64,4672]{2,1,0:T(8,128)(2,1)} %param.12) | copy-start | bytes 3588100
  141.2 116.7 %all-gather.7.cloned.1.call-start = ((), (), s32[]{:S(2)}) async-start(), calls=%async_computation.6 | async-start | bytes 10911744 | tf_op jit(solution)/shard_map/all_gather | solution.py:60
  205.2 179.0 %reduce-scatter.7.cloned.1.call-start = ((), (), s32[]{:S(2)}) async-start(), calls=%async_computation.7 | async-start | bytes 10911744 | tf_op jit(solution)/shard_map/reduce_scatter | solution.py:65
  257.9 24.1 %copy-start.10 = (bf16[2,512,4672]{2,1,0:T(8,128)(2,1)S(1)}, bf16[2,512,4672]{2,1,0:T(8,128)(2,1)}, u32[]{:S(2)}) copy-start(bf16[2,512,4672]{2,1,0:T(8,128)(2,1)} %all-gather.7.cloned.1.call-done) | copy-start | bytes 28704772
  329.0 57.6 %copy-start.4 = (f32[4672]{0:T(1024)S(1)}, f32[4672]{0:T(1024)}, u32[]{:S(2)}) copy-start(f32[4672]{0:T(1024)} %get-tuple-element.5) | copy-start | bytes 56068
  329.0 111.6 %all-gather.9.cloned.1.call-start = ((), (), s32[]{:S(2)}) async-start(), calls=%async_computation.8 | async-start | bytes 10911744 | tf_op jit(solution)/shard_map/all_gather | solution.py:49
  388.0 160.5 %reduce-scatter.9.cloned.1.call-start = ((), (), s32[]{:S(2)}) async-start(), calls=%async_computation.9 | async-start | bytes 10911744 | tf_op jit(solution)/shard_map/reduce_scatter | solution.py:58
  440.7 9.6 %copy-start.9 = (bf16[2,512,4672]{2,1,0:T(8,128)(2,1)S(1)}, bf16[2,512,4672]{2,1,0:T(8,128)(2,1)}, u32[]{:S(2)}) copy-start(bf16[2,512,4672]{2,1,0:T(8,128)(2,1)} %all-gather.9.cloned.1.call-done) | copy-start | bytes 28704772
  450.3 7.4 copy-start.3
  493.2 57.0 %copy-start.5 = (f32[4672]{0:T(1024)S(1)}, f32[4672]{0:T(1024)}, u32[]{:S(2)}) copy-start(f32[4672]{0:T(1024)} %get-tuple-element.8) | copy-start | bytes 56068
  493.3 112.4 %all-gather.11.cloned.1.call-start = ((), (), s32[]{:S(2)}) async-start(), calls=%async_computation.10 | async-start | bytes 10911744 | tf_op jit(solution)/shard_map/all_gather | solution.py:60
  553.1 178.0 %reduce-scatter.11.cloned.1.call-start = ((), (), s32[]{:S(2)}) async-start(), calls=%async_computation.11 | async-start | bytes 10911744 | tf_op jit(solution)/shard_map/reduce_scatter | solution.py:65
  605.7 24.3 %copy-start.11 = (bf16[2,512,4672]{2,1,0:T(8,128)(2,1)S(1)}, bf16[2,512,4672]{2,1,0:T(8,128)(2,1)}, u32[]{:S(2)}) copy-start(bf16[2,512,4672]{2,1,0:T(8,128)(2,1)} %all-gather.11.cloned.1.call-done) | copy-start | bytes 28704772
  675.8 55.3 %copy-start.1 = (bf16[2,64,4672]{2,1,0:T(8,128)(2,1)S(1)}, bf16[2,64,4672]{2,1,0:T(8,128)(2,1)}, u32[]{:S(2)}) copy-start(bf16[2,64,4672]{2,1,0:T(8,128)(2,1)} %reduce-scatter.9.cloned.1.call-done) | copy-start | bytes 3588100
Sparse Core Ops, SparseCore 0:
  12.6 56.5 all-gather.4
  141.3 59.3 reduce-scatter.4
  205.4 52.4 all-gather.6
  329.2 55.0 reduce-scatter.6
  388.1 52.5 all-gather.8
  493.4 55.0 reduce-scatter.8
  553.2 52.4 all-gather.10
  676.0 55.0 reduce-scatter.10
where the time goes:
time: 751 us; the launch traced here: 741 us
  waiting for transfers between devices  374 us (50%)
  matrix products  246 us (33%)
  local copies, waits for them, and re-layouts  85.6 us (11%)
  other arithmetic  20.1 us (3%)
  between operations  14.2 us (2%)
    reduce_scatter x2, waiting for transfers between devices, local_fn(): attn_out = lax.psum_scatter(part_out, 'tp', scatter_dimension=1, tiled=True)  113 us
    reduce_scatter x2, waiting for transfers between devices, local_fn(): ffn_out = lax.psum_scatter(part_out, 'tp', scatter_dimension=1, tiled=True)  110 us
    all_gather x2, waiting for transfers between devices, local_fn(): lax.all_gather(rms_norm(mid_resid, norm_mlp[layer_idx]), 'tp', axis=1, ti...  105 us
    dot_general x6, matrix products, project(): jnp.einsum('bsd,dn->bsn', gathered, weight_mat, preferred_element_type=jn...  53.1 us
    dot_general x2, matrix products, local_fn(): jnp.einsum('bsf,fd->bsd', gated, w_down[layer_idx], preferred_element_typ...  50 us
    dot_general x2, matrix products, local_fn(): jnp.einsum('bsd,df->bsf', gathered, w_lin[layer_idx], preferred_element_t...  48.3 us
    all_gather x2, waiting for transfers between devices, local_fn(): lax.all_gather(rms_norm(residual, norm_attn[layer_idx]), 'tp', axis=1, ti...  45.2 us
    dot_general x2, matrix products, local_fn(): jnp.einsum('bsd,df->bsf', gathered, w_act[layer_idx], preferred_element_t...  42.9 us
  transfers between devices with their start and end apart: 8, of which 7 were waited for; matrix products, arithmetic and copies ran while one was open for 11% of the time, Pallas kernels for 0%

commit v1 on v0

v1 whole, which is shorter than its diff:
```python
import functools

import jax
import jax.numpy as jnp
from jax import lax
from jax.experimental import pallas as pl
from jax.experimental.pallas import tpu as pltpu
from jax.sharding import PartitionSpec as P


def rms_norm(rows_in, gain_vec):
    rows32 = rows_in.astype(jnp.float32)
    inv_rms = lax.rsqrt(jnp.mean(rows32 * rows32, axis=-1, keepdims=True) + 1e-6)
    return (rows32 * inv_rms * gain_vec).astype(jnp.bfloat16)


def bias_kernel(seq_len, table_ref, bias_ref):
    head_count = table_ref.shape[0]
    offsets = lax.broadcasted_iota(jnp.int32, (head_count, 2 * seq_len), 1) - seq_len
    distance = jnp.minimum(jnp.abs(offsets), 128)
    bucket = jnp.full_like(distance, 8)
    for step in range(1, 8):
        bucket = bucket + (distance * distance >= 64 * 2 ** step).astype(jnp.int32)
    bucket = jnp.where(distance < 8, distance, bucket) + jnp.where(offsets > 0, 16, 0)
    values = jnp.zeros((head_count, 2 * seq_len), jnp.float32)
    for index in range(table_ref.shape[1]):
        values = jnp.where(bucket == index, table_ref[:, index:index + 1], values)
    for head in range(head_count):
        wide = jnp.broadcast_to(values[head:head + 1], (seq_len, 2 * seq_len))
        bias_ref[head] = pltpu.roll(wide, 0, 1, stride=1, stride_axis=0)[:, seq_len:]


def solution(mesh):
    group_size = mesh.shape['tp']
    col_spec = P(None, None, 'tp')
    row_spec = P(None, 'tp', None)

    def local_fn(tokens, pad_mask, rel_table, w_query, w_key, w_value, w_out, w_act, w_lin, w_down, norm_attn, norm_mlp):
        batch, seq_loc, model_dim = tokens.shape
        seq_len = seq_loc * group_size
        head_count = rel_table.shape[1]
        head_dim = w_query.shape[2] // head_count
        rel_bias = pl.pallas_call(
            functools.partial(bias_kernel, seq_len),
            out_shape=jax.ShapeDtypeStruct((head_count, seq_len, seq_len), jnp.float32),
            name='rel_bias',
        )(rel_table.T)
        key_bias = jnp.where(pad_mask == 1, 0.0, -1e9).astype(jnp.float32)

        def project(gathered, weight_mat):
            projected = jnp.dot(gathered, weight_mat, preferred_element_type=jnp.float32)
            return projected.astype(jnp.bfloat16).reshape(seq_len, head_count, head_dim)

        streams = [tokens[row] for row in range(batch)]
        for layer_idx in range(w_query.shape[0]):
            for row in range(batch):
                residual = streams[row]
                gathered = lax.all_gather(rms_norm(residual, norm_attn[layer_idx]), 'tp', axis=0, tiled=True)
                query_proj = project(gathered, w_query[layer_idx])
                key_proj = project(gathered, w_key[layer_idx])
                value_proj = project(gathered, w_value[layer_idx])
                scores = jnp.einsum('qhe,khe->hqk', query_proj, key_proj, preferred_element_type=jnp.float32)
                attn_probs = jax.nn.softmax(scores + rel_bias + key_bias[row], axis=-1).astype(jnp.bfloat16)
                context = jnp.einsum('hqk,khe->qhe', attn_probs, value_proj, preferred_element_type=jnp.float32).astype(jnp.bfloat16)
                part_out = jnp.dot(context.reshape(seq_len, head_count * head_dim), w_out[layer_idx], preferred_element_type=jnp.float32).astype(jnp.bfloat16)
                attn_out = lax.psum_scatter(part_out, 'tp', scatter_dimension=0, tiled=True)
                streams[row] = (residual.astype(jnp.float32) + attn_out.astype(jnp.float32)).astype(jnp.bfloat16)
            for row in range(batch):
                residual = streams[row]
                gathered = lax.all_gather(rms_norm(residual, norm_mlp[layer_idx]), 'tp', axis=0, tiled=True)
                act_proj = jnp.dot(gathered, w_act[layer_idx], preferred_element_type=jnp.float32)
                lin_proj = jnp.dot(gathered, w_lin[layer_idx], preferred_element_type=jnp.float32)
                gated = (jax.nn.gelu(act_proj, approximate=True) * lin_proj).astype(jnp.bfloat16)
                part_out = jnp.dot(gated, w_down[layer_idx], preferred_element_type=jnp.float32).astype(jnp.bfloat16)
                ffn_out = lax.psum_scatter(part_out, 'tp', scatter_dimension=0, tiled=True)
                streams[row] = (residual.astype(jnp.float32) + ffn_out.astype(jnp.float32)).astype(jnp.bfloat16)
        return jnp.stack(streams)

    in_specs = (P('dp', 'tp', None), P('dp', None), P(None, 'tp'), col_spec, col_spec, col_spec, row_spec,
                col_spec, col_spec, row_spec, P(None, None), P(None, None))
    return jax.shard_map(local_fn, mesh=mesh, in_specs=in_specs, out_specs=P('dp', 'tp', None), check_vma=False)
```

time: 751 us -> 673 us (0.90)
  waiting for transfers between devices: 374 us -> 260 us
  matrix products: 246 us -> 342 us
  local copies, waits for them, and re-layouts: 85.6 us -> 3.95 us
  other arithmetic: 20.1 us -> 34.3 us
    dot_general x14 -> x32, matrix products: 223 us -> 342 us  [the longest x4 110 us: local_fn(): jnp.dot(gated, w_down[layer_idx], preferred_element_type=jnp.float32)]
    reduce_scatter x4 -> x8, waiting for transfers between devices: 224 us -> 128 us  [the longest x4 64.3 us: local_fn(): ffn_out = lax.psum_scatter(part_out, 'tp', scatter_dimension=0, tiled=True)]
    slice x6 -> x1, local copies, waits for them, and re-layouts: 47.4 us -> 0.01 us  [local_fn(): key_bias[row]]
    sub x2 -> x0, matrix products: 23.3 us -> none  [local_fn(): jax.nn.softmax(scores + rel_bias + key_bias, axis=-1).astype(jnp.bfloat16)]
    all_gather x4 -> x8, waiting for transfers between devices: 150 us -> 129 us  [the longest x4 66.2 us: local_fn(): lax.all_gather(rms_norm(residual, norm_mlp[layer_idx]), 'tp', axis=0, til...]
    reshape x1 -> x0, local copies, waits for them, and re-layouts: 17.2 us -> none  [bias_rows(): tiled.reshape(dist_table.shape[0], row_count, 2 * seq_len - 1)]
    sub x0 -> x4, other arithmetic: none -> 12.8 us  [local_fn(): jax.nn.softmax(scores + rel_bias + key_bias[row], axis=-1)]
    unnamed x27 -> x56, local copies, waits for them, and re-layouts: 13.7 us -> 1.72 us
  transfers between devices with their start and end apart: 8 -> 16, of which waited for: 7 -> 8; matrix products, arithmetic and copies ran while one was open for 11% -> 54% of each run, Pallas kernels for 0% -> 1%
where the time goes in v1:
time: 673 us; the launch traced here: 661 us
  matrix products  342 us (51%)
  waiting for transfers between devices  260 us (39%)
  other arithmetic  34.3 us (5%)
  between operations  14.2 us (2%)
    dot_general x4, matrix products, local_fn(): jnp.dot(gated, w_down[layer_idx], preferred_element_type=jnp.float32)  110 us
    dot_general x12, matrix products, project(): jnp.dot(gathered, weight_mat, preferred_element_type=jnp.float32)  88.1 us
    all_gather x4, waiting for transfers between devices, local_fn(): lax.all_gather(rms_norm(residual, norm_mlp[layer_idx]), 'tp', axis=0, til...  66.2 us
    reduce_scatter x4, waiting for transfers between devices, local_fn(): ffn_out = lax.psum_scatter(part_out, 'tp', scatter_dimension=0, tiled=True)  64.3 us
    reduce_scatter x4, waiting for transfers between devices, local_fn(): attn_out = lax.psum_scatter(part_out, 'tp', scatter_dimension=0, tiled=True)  63.8 us
    all_gather x4, waiting for transfers between devices, local_fn(): lax.all_gather(rms_norm(residual, norm_attn[layer_idx]), 'tp', axis=0, ti...  62.6 us
    dot_general x4, matrix products, local_fn(): jnp.dot(gathered, w_act[layer_idx], preferred_element_type=jnp.float32)  57.8 us
    dot_general x4, matrix products, local_fn(): jnp.einsum('hqk,khe->qhe', attn_probs, value_proj, preferred_element_type...  53.6 us
  transfers between devices with their start and end apart: 16, of which 8 were waited for; matrix products, arithmetic and copies ran while one was open for 54% of the time, Pallas kernels for 1%

profile of v1, /device:TPU:81, one launch (start us, length us, event | category | flops | bytes accessed | tf_op | source)
XLA Modules:
  0.0 661.3 jit_solution(14610138831873837023)
XLA Ops:
  6.6 1.6 fusion.232
  8.1 1.6 slice_reduce_fusion.1
  9.7 2.7 fusion.238
  12.5 0.7 all-gather.17.cloned.1.call-update
  13.3 5.2 rel_bias.1
  18.6 30.0 %all-gather.9.cloned.1.call-done = bf16[512,4672]{1,0:T(8,128)(2,1)} async-done(((bf16[64,4672]{1,0:T(8,128)(2,1)}), bf16[512,4672]{1,0:T(8,128)(2,1)}) %all-gather.9.cloned.1.call-update) | async-done | bytes 4784144 | tf_op jit(solution)/shard_map/all_gather | solution.py:58
  48.5 6.7 %fusion.178 = bf16[512,512]{0,1:T(8,128)(2,1)S(1)} fusion(bf16[512,4672]{1,0:T(8,128)(2,1)} %all-gather.9.cloned.1.call-done, bf16[2,4672,512]{2,1,0:T(8,128)(2,1)} %param.15), kind=kOutput, calls=%fused_computation.178 | convolution fusion | flops 2449735680 | bytes 10158080 | tf_op jit(solution)/shard_map/dot_general | solution.py:51
  55.3 5.3 fusion.184
  60.6 1.3 add_add_fusion.3
  61.9 3.2 fusion.249
  65.2 19.1 %fusion.172 = bf16[512,512]{0,1:T(8,128)(2,1)S(1)} fusion(bf16[512,4672]{1,0:T(8,128)(2,1)} %all-gather.9.cloned.1.call-done, bf16[2,4672,512]{2,1,0:T(8,128)(2,1)} %param.17), kind=kOutput, calls=%fused_computation.176 | convolution fusion | flops 2449735680 | bytes 10158080 | tf_op jit(solution)/shard_map/dot_general | solution.py:51
  84.3 13.5 %fusion.171 = bf16[8,64,512]{2,1,0:T(8,128)(2,1)S(1)} fusion(bf16[512,8,64]{0,2,1:T(8,128)(2,1)S(1)} %bitcast.254, f32[8,512]{1,0:T(8,128)S(1)} %fusion.249, f32[8,512,512]{2,1,0:T(8,128)} %copy-done.2), kind=kOutput, calls=%fused_computation.175 | convolution fusion | flops 274993664 | bytes 9453568 | tf_op jit(solution)/shard_map/hqk,khe->qhe/dot_general | solution.py:64
  97.7 6.9 %convolution_convert_fusion.3 = bf16[512,4672]{1,0:T(8,128)(2,1)} fusion(bf16[512,512]{0,1:T(8,128)(2,1)S(1)} %bitcast.255, bf16[2,512,4672]{1,2,0:T(8,128)(2,1)} %param.18), kind=kOutput, calls=%fused_computation.59 | convolution fusion | flops 2451865600 | bytes 10092544 | tf_op jit(solution)/shard_map/dot_general | solution.py:65
  104.8 6.7 %fusion.181 = bf16[512,512]{0,1:T(8,128)(2,1)S(1)} fusion(bf16[512,4672]{1,0:T(8,128)(2,1)} %all-gather.17.cloned.1.call-done, bf16[2,4672,512]{2,1,0:T(8,128)(2,1)} %param.15), kind=kOutput, calls=%fused_computation.179 | convolution fusion | flops 2449735680 | bytes 10158080 | tf_op jit(solution)/shard_map/dot_general | solution.py:51
  111.5 5.3 fusion.187
  116.9 1.3 add_add_fusion.1
  118.2 3.2 fusion.250
  121.4 7.0 %fusion.175 = bf16[512,512]{0,1:T(8,128)(2,1)S(1)} fusion(bf16[512,4672]{1,0:T(8,128)(2,1)} %all-gather.17.cloned.1.call-done, bf16[2,4672,512]{2,1,0:T(8,128)(2,1)} %param.17), kind=kOutput, calls=%fused_computation.177 | convolution fusion | flops 2449735680 | bytes 10158080 | tf_op jit(solution)/shard_map/dot_general | solution.py:51
  128.5 13.5 %fusion.169 = bf16[8,64,512]{2,1,0:T(8,128)(2,1)S(1)} fusion(bf16[512,8,64]{0,2,1:T(8,128)(2,1)S(1)} %bitcast.256, f32[8,512]{1,0:T(8,128)S(1)} %fusion.250, f32[8,512,512]{2,1,0:T(8,128)} %copy-done.3), kind=kOutput, calls=%fused_computation.173 | convolution fusion | flops 274993664 | bytes 9453568 | tf_op jit(solution)/shard_map/hqk,khe->qhe/dot_general | solution.py:64
  141.9 6.9 %convolution_convert_fusion.1 = bf16[512,4672]{1,0:T(8,128)(2,1)} fusion(bf16[512,512]{0,1:T(8,128)(2,1)S(1)} %bitcast.257, bf16[2,512,4672]{1,2,0:T(8,128)(2,1)} %param.18), kind=kOutput, calls=%fused_computation.57 | convolution fusion | flops 2451865600 | bytes 10092544 | tf_op jit(solution)/shard_map/dot_general | solution.py:65
  149.0 0.6 copy-done.10
  149.6 0.7 slice_reduce_fusion
  150.3 32.0 %reduce-scatter.17.cloned.1.call-done = bf16[64,4672]{1,0:T(8,128)(2,1)} async-done(((bf16[512,4672]{1,0:T(8,128)(2,1)}), bf16[64,4672]{1,0:T(8,128)(2,1)}) %reduce-scatter.17.cloned.1.call-update) | async-done | bytes 598032 | tf_op jit(solution)/shard_map/reduce_scatter | solution.py:66
  182.2 1.7 fusion.208
  184.0 2.7 fusion.210
  186.9 0.6 all-gather.19.cloned.1.call-update
  187.5 33.1 %all-gather.11.cloned.1.call-done = bf16[512,4672]{1,0:T(8,128)(2,1)} async-done(((bf16[64,4672]{1,0:T(8,128)(2,1)}), bf16[512,4672]{1,0:T(8,128)(2,1)}) %all-gather.11.cloned.1.call-update) | async-done | bytes 4784144 | tf_op jit(solution)/shard_map/all_gather | solution.py:70
  220.6 14.4 %fusion.118 = f32[512,1544]{0,1:T(8,128)} fusion(bf16[512,4672]{1,0:T(8,128)(2,1)} %all-gather.11.cloned.1.call-done, bf16[2,4672,1544]{1,2,0:T(8,128)(2,1)} %param.19), kind=kOutput, calls=%fused_computation.122 | convolution fusion | flops 7393017856 | bytes 22636544 | tf_op jit(solution)/shard_map/dot_general | solution.py:71
  235.0 27.5 %fusion.40 = bf16[512,4672]{1,0:T(8,128)(2,1)} fusion(bf16[2,1544,4672]{2,1,0:T(8,128)(2,1)} %param.21, f32[512,1544]{0,1:T(8,128)} %fusion.118, bf16[512,4672]{1,0:T(8,128)(2,1)} %all-gather.11.cloned.1.call-done, bf16[2,4672,1544]{1,2,0:T(8,128)(2,1)} %param.20), kind=kOutput, calls=%fused_computation.52 | convolution fusion | flops 14777360384 | bytes 42045440 | tf_op jit(solution)/shard_map/dot_general | solution.py:74
  262.8 14.5 %fusion.136 = f32[512,1544]{0,1:T(8,128)} fusion(bf16[512,4672]{1,0:T(8,128)(2,1)} %all-gather.19.cloned.1.call-done, bf16[2,4672,1544]{1,2,0:T(8,128)(2,1)} %param.19), kind=kOutput, calls=%fused_computation.136 | convolution fusion | flops 7393017856 | bytes 22636544 | tf_op jit(solution)/shard_map/dot_general | solution.py:71
  277.3 27.4 %fusion.43 = bf16[512,4672]{1,0:T(8,128)(2,1)} fusion(bf16[2,1544,4672]{2,1,0:T(8,128)(2,1)} %param.21, f32[512,1544]{0,1:T(8,128)} %fusion.136, bf16[512,4672]{1,0:T(8,128)(2,1)} %all-gather.19.cloned.1.call-done, bf16[2,4672,1544]{1,2,0:T(8,128)(2,1)} %param.20), kind=kOutput, calls=%fused_computation.53 | convolution fusion | flops 14777360384 | bytes 42045440 | tf_op jit(solution)/shard_map/dot_general | solution.py:74
  304.8 33.2 %reduce-scatter.19.cloned.1.call-done = bf16[64,4672]{1,0:T(8,128)(2,1)} async-done(((bf16[512,4672]{1,0:T(8,128)(2,1)}), bf16[64,4672]{1,0:T(8,128)(2,1)}) %reduce-scatter.19.cloned.1.call-update) | async-done | bytes 598032 | tf_op jit(solution)/shard_map/reduce_scatter | solution.py:75
  338.0 2.1 fusion.212
  340.2 1.4 fusion.214
  341.7 0.6 all-gather.21.cloned.1.call-update
  342.7 32.6 %all-gather.13.cloned.1.call-done = bf16[512,4672]{1,0:T(8,128)(2,1)} async-done(((bf16[64,4672]{1,0:T(8,128)(2,1)}), bf16[512,4672]{1,0:T(8,128)(2,1)}) %all-gather.13.cloned.1.call-update) | async-done | bytes 4784144 | tf_op jit(solution)/shard_map/all_gather | solution.py:58
  375.3 6.7 %fusion.196 = bf16[512,512]{0,1:T(8,128)(2,1)S(1)} fusion(bf16[512,4672]{1,0:T(8,128)(2,1)} %all-gather.13.cloned.1.call-done, bf16[2,4672,512]{2,1,0:T(8,128)(2,1)} %param.15), kind=kOutput, calls=%fused_computation.184 | convolution fusion | flops 2449735680 | bytes 10158080 | tf_op jit(solution)/shard_map/dot_general | solution.py:51
  382.1 5.3 fusion.202
  387.4 1.3 add_add_fusion.2
  388.8 3.2 fusion.251
  392.0 6.8 %fusion.190 = bf16[512,512]{0,1:T(8,128)(2,1)S(1)} fusion(bf16[512,4672]{1,0:T(8,128)(2,1)} %all-gather.13.cloned.1.call-done, bf16[2,4672,512]{2,1,0:T(8,128)(2,1)} %param.17), kind=kOutput, calls=%fused_computation.182 | convolution fusion | flops 2449735680 | bytes 10158080 | tf_op jit(solution)/shard_map/dot_general | solution.py:51
  398.8 13.5 %fusion.170 = bf16[8,64,512]{2,1,0:T(8,128)(2,1)S(1)} fusion(bf16[512,8,64]{0,2,1:T(8,128)(2,1)S(1)} %bitcast.258, f32[8,512]{1,0:T(8,128)S(1)} %fusion.251, f32[8,512,512]{2,1,0:T(8,128)} %copy-done.1), kind=kOutput, calls=%fused_computation.174 | convolution fusion | flops 274993664 | bytes 9453568 | tf_op jit(solution)/shard_map/hqk,khe->qhe/dot_general | solution.py:64
  412.3 6.9 %convolution_convert_fusion.2 = bf16[512,4672]{1,0:T(8,128)(2,1)} fusion(bf16[512,512]{0,1:T(8,128)(2,1)S(1)} %bitcast.259, bf16[2,512,4672]{1,2,0:T(8,128)(2,1)} %param.18), kind=kOutput, calls=%fused_computation.58 | convolution fusion | flops 2451865600 | bytes 10092544 | tf_op jit(solution)/shard_map/dot_general | solution.py:65
  419.3 6.7 %fusion.199 = bf16[512,512]{0,1:T(8,128)(2,1)S(1)} fusion(bf16[512,4672]{1,0:T(8,128)(2,1)} %all-gather.21.cloned.1.call-done, bf16[2,4672,512]{2,1,0:T(8,128)(2,1)} %param.15), kind=kOutput, calls=%fused_computation.185 | convolution fusion | flops 2449735680 | bytes 10158080 | tf_op jit(solution)/shard_map/dot_general | solution.py:51
  426.1 5.3 fusion.205
  431.5 1.3 add_add_fusion
  432.8 3.2 fusion.252
  436.0 7.0 %fusion.193 = bf16[512,512]{0,1:T(8,128)(2,1)S(1)} fusion(bf16[512,4672]{1,0:T(8,128)(2,1)} %all-gather.21.cloned.1.call-done, bf16[2,4672,512]{2,1,0:T(8,128)(2,1)} %param.17), kind=kOutput, calls=%fused_computation.183 | convolution fusion | flops 2449735680 | bytes 10158080 | tf_op jit(solution)/shard_map/dot_general | solution.py:51
  443.0 13.2 %fusion.168 = bf16[8,64,512]{2,1,0:T(8,128)(2,1)S(1)} fusion(bf16[512,8,64]{0,2,1:T(8,128)(2,1)S(1)} %bitcast.260, f32[8,512]{1,0:T(8,128)S(1)} %fusion.252, f32[8,512,512]{2,1,0:T(8,128)} %copy-done), kind=kOutput, calls=%fused_computation.172 | convolution fusion | flops 274993664 | bytes 9453568 | tf_op jit(solution)/shard_map/hqk,khe->qhe/dot_general | solution.py:64
  456.2 7.0 %convolution_convert_fusion = bf16[512,4672]{1,0:T(8,128)(2,1)} fusion(bf16[512,512]{0,1:T(8,128)(2,1)S(1)} %bitcast.261, bf16[2,512,4672]{1,2,0:T(8,128)(2,1)} %param.18), kind=kOutput, calls=%fused_computation.56 | convolution fusion | flops 2451865600 | bytes 10092544 | tf_op jit(solution)/shard_map/dot_general | solution.py:65
  463.4 1.4 fusion.216
  464.8 31.8 %reduce-scatter.21.cloned.1.call-done = bf16[64,4672]{1,0:T(8,128)(2,1)} async-done(((bf16[512,4672]{1,0:T(8,128)(2,1)}), bf16[64,4672]{1,0:T(8,128)(2,1)}) %reduce-scatter.21.cloned.1.call-update) | async-done | bytes 598032 | tf_op jit(solution)/shard_map/reduce_scatter | solution.py:66
  496.6 1.4 fusion.228
  498.0 2.8 fusion.218
  501.5 33.1 %all-gather.23.cloned.1.call-done = bf16[512,4672]{1,0:T(8,128)(2,1)} async-done(((bf16[64,4672]{1,0:T(8,128)(2,1)}), bf16[512,4672]{1,0:T(8,128)(2,1)}) %all-gather.23.cloned.1.call-update) | async-done | bytes 4784144 | tf_op jit(solution)/shard_map/all_gather | solution.py:70
  534.6 14.4 %fusion.145 = f32[512,1544]{0,1:T(8,128)} fusion(bf16[512,4672]{1,0:T(8,128)(2,1)} %all-gather.23.cloned.1.call-done, bf16[2,4672,1544]{1,2,0:T(8,128)(2,1)} %param.19), kind=kOutput, calls=%fused_computation.143 | convolution fusion | flops 7393017856 | bytes 22636544 | tf_op jit(solution)/shard_map/dot_general | solution.py:71
  549.0 27.5 %fusion.49 = bf16[512,4672]{1,0:T(8,128)(2,1)} fusion(bf16[2,1544,4672]{2,1,0:T(8,128)(2,1)} %param.21, f32[512,1544]{0,1:T(8,128)} %fusion.145, bf16[512,4672]{1,0:T(8,128)(2,1)} %all-gather.23.cloned.1.call-done, bf16[2,4672,1544]{1,2,0:T(8,128)(2,1)} %param.20), kind=kOutput, calls=%fused_computation.55 | convolution fusion | flops 14777360384 | bytes 42045440 | tf_op jit(solution)/shard_map/dot_general | solution.py:74
  576.9 14.5 %fusion.127 = f32[512,1544]{0,1:T(8,128)} fusion(bf16[512,4672]{1,0:T(8,128)(2,1)} %all-gather.15.cloned.1.call-done, bf16[2,4672,1544]{1,2,0:T(8,128)(2,1)} %param.19), kind=kOutput, calls=%fused_computation.129 | convolution fusion | flops 7393017856 | bytes 22636544 | tf_op jit(solution)/shard_map/dot_general | solution.py:71
  591.3 27.4 %fusion.46 = bf16[512,4672]{1,0:T(8,128)(2,1)} fusion(bf16[2,1544,4672]{2,1,0:T(8,128)(2,1)} %param.21, f32[512,1544]{0,1:T(8,128)} %fusion.127, bf16[512,4672]{1,0:T(8,128)(2,1)} %all-gather.15.cloned.1.call-done, bf16[2,4672,1544]{1,2,0:T(8,128)(2,1)} %param.20), kind=kOutput, calls=%fused_computation.54 | convolution fusion | flops 14777360384 | bytes 42045440 | tf_op jit(solution)/shard_map/dot_general | solution.py:74
  618.8 1.0 copy-done.6
  619.8 1.3 fusion.240
  621.1 31.0 %reduce-scatter.15.cloned.1.call-done = bf16[64,4672]{1,0:T(8,128)(2,1)} async-done(((bf16[512,4672]{1,0:T(8,128)(2,1)}), bf16[64,4672]{1,0:T(8,128)(2,1)}) %reduce-scatter.15.cloned.1.call-update) | async-done | bytes 598032 | tf_op jit(solution)/shard_map/reduce_scatter | solution.py:75
  652.1 1.3 fusion.241
  653.4 1.2 pad_maximum_fusion
  (104 shorter events, 3.2 us)
Async XLA Ops:
  6.5 42.0 %all-gather.9.cloned.1.call-start = ((), (), s32[]{:S(2)}) async-start(), calls=%async_computation.8 | async-start | bytes 5455872 | tf_op jit(solution)/shard_map/all_gather | solution.py:58
  12.4 6.1 copy-start.15
  12.5 92.3 %all-gather.17.cloned.1.call-start = ((), (), s32[]{:S(2)}) async-start(), calls=%async_computation.16 | async-start | bytes 5455872 | tf_op jit(solution)/shard_map/all_gather | solution.py:58
  13.3 137.0 %reduce-scatter.9.cloned.1.call-start = ((), (), s32[]{:S(2)}) async-start(), calls=%async_computation.9 | async-start | bytes 5455872 | tf_op jit(solution)/shard_map/reduce_scatter | solution.py:66
  18.5 42.1 %copy-start.13 = (f32[1,512]{1,0:T(1,128)}, f32[1,512]{1,0:T(1,128)S(1)}, u32[]{:S(2)}) copy-start(f32[1,512]{1,0:T(1,128)S(1)} %get-tuple-element.28) | copy-start | bytes 6148
  18.5 98.3 %copy-start.11 = (f32[1,512]{1,0:T(1,128)}, f32[1,512]{1,0:T(1,128)S(1)}, u32[]{:S(2)}) copy-start(f32[1,512]{1,0:T(1,128)S(1)} %get-tuple-element.27) | copy-start | bytes 6148
  48.5 6.7 %copy-start.18 = (bf16[512,4672]{1,0:T(8,128)(2,1)S(1)}, bf16[512,4672]{1,0:T(8,128)(2,1)}, u32[]{:S(2)}) copy-start(bf16[512,4672]{1,0:T(8,128)(2,1)} %all-gather.9.cloned.1.call-done) | copy-start | bytes 14352388
  48.5 12.1 %slice-start = ((s8[8388608]{0:T(1024)(128)(4,1)}), s8[4194304]{0:T(1024)(128)(4,1)S(1)}, s32[]{:S(2)}) async-start(s8[8388608]{0:T(1024)(128)(4,1)} %bitcast.233), calls=%async_computation.24 | async-start | bytes 8388608
  55.3 5.3 slice-start.1
  61.9 22.3 %copy-start.2 = (f32[8,512,512]{2,1,0:T(8,128)}, f32[8,512,512]{2,1,0:T(8,128)S(1)}, u32[]{:S(2)}) copy-start(f32[8,512,512]{2,1,0:T(8,128)S(1)} %add_add_fusion.3) | copy-start | bytes 25165828
  104.7 77.6 %reduce-scatter.17.cloned.1.call-start = ((), (), s32[]{:S(2)}) async-start(), calls=%async_computation.17 | async-start | bytes 5455872 | tf_op jit(solution)/shard_map/reduce_scatter | solution.py:66
  104.7 6.8 %copy-start.16 = (bf16[512,4672]{1,0:T(8,128)(2,1)S(1)}, bf16[512,4672]{1,0:T(8,128)(2,1)}, u32[]{:S(2)}) copy-start(bf16[512,4672]{1,0:T(8,128)(2,1)} %all-gather.17.cloned.1.call-done) | copy-start | bytes 14352388
  104.8 12.1 %slice-start.2 = ((s8[8388608]{0:T(1024)(128)(4,1)}), s8[4194304]{0:T(1024)(128)(4,1)S(1)}, s32[]{:S(2)}) async-start(s8[8388608]{0:T(1024)(128)(4,1)} %bitcast.235), calls=%async_computation.26 | async-start | bytes 8388608
  111.5 5.3 slice-start.3
  118.2 10.3 %copy-start.3 = (f32[8,512,512]{2,1,0:T(8,128)}, f32[8,512,512]{2,1,0:T(8,128)S(1)}, u32[]{:S(2)}) copy-start(f32[8,512,512]{2,1,0:T(8,128)S(1)} %add_add_fusion.1) | copy-start | bytes 25165828
  148.8 0.8 copy-start.10
  148.8 33.4 %copy-start.4 = (bf16[2,64,4672]{2,1,0:T(8,128)(2,1)S(1)}, bf16[2,64,4672]{2,1,0:T(8,128)(2,1)}, u32[]{:S(2)}) copy-start(bf16[2,64,4672]{2,1,0:T(8,128)(2,1)} %param.12) | copy-start | bytes 3588100
  148.9 71.7 %all-gather.11.cloned.1.call-start = ((), (), s32[]{:S(2)}) async-start(), calls=%async_computation.10 | async-start | bytes 5455872 | tf_op jit(solution)/shard_map/all_gather | solution.py:70
  186.8 76.0 %all-gather.19.cloned.1.call-start = ((), (), s32[]{:S(2)}) async-start(), calls=%async_computation.18 | async-start | bytes 5455872 | tf_op jit(solution)/shard_map/all_gather | solution.py:70
  187.4 117.4 %reduce-scatter.11.cloned.1.call-start = ((), (), s32[]{:S(2)}) async-start(), calls=%async_computation.11 | async-start | bytes 5455872 | tf_op jit(solution)/shard_map/reduce_scatter | solution.py:75
  262.5 75.5 %reduce-scatter.19.cloned.1.call-start = ((), (), s32[]{:S(2)}) async-start(), calls=%async_computation.19 | async-start | bytes 5455872 | tf_op jit(solution)/shard_map/reduce_scatter | solution.py:75
  304.6 33.4 %copy-start.7 = (bf16[64,4672]{1,0:T(8,128)(2,1)S(1)}, bf16[64,4672]{1,0:T(8,128)(2,1)}, u32[]{:S(2)}) copy-start(bf16[64,4672]{1,0:T(8,128)(2,1)} %reduce-scatter.9.cloned.1.call-done) | copy-start | bytes 1794052
  304.6 35.5 %copy-start.9 = (f32[4672]{0:T(1024)S(1)}, f32[4672]{0:T(1024)}, u32[]{:S(2)}) copy-start(f32[4672]{0:T(1024)} %get-tuple-element.11) | copy-start | bytes 56068
  304.7 70.6 %all-gather.13.cloned.1.call-start = ((), (), s32[]{:S(2)}) async-start(), calls=%async_computation.12 | async-start | bytes 5455872 | tf_op jit(solution)/shard_map/all_gather | solution.py:58
  341.6 77.7 %all-gather.21.cloned.1.call-start = ((), (), s32[]{:S(2)}) async-start(), calls=%async_computation.20 | async-start | bytes 5455872 | tf_op jit(solution)/shard_map/all_gather | solution.py:58
  342.3 121.1 %reduce-scatter.13.cloned.1.call-start = ((), (), s32[]{:S(2)}) async-start(), calls=%async_computation.13 | async-start | bytes 5455872 | tf_op jit(solution)/shard_map/reduce_scatter | solution.py:66
  375.3 6.7 %copy-start.19 = (bf16[512,4672]{1,0:T(8,128)(2,1)S(1)}, bf16[512,4672]{1,0:T(8,128)(2,1)}, u32[]{:S(2)}) copy-start(bf16[512,4672]{1,0:T(8,128)(2,1)} %all-gather.13.cloned.1.call-done) | copy-start | bytes 14352388
  375.3 12.1 %slice-start.4 = ((s8[8388608]{0:T(1024)(128)(4,1)}), s8[4194304]{0:T(1024)(128)(4,1)S(1)}, s32[]{:S(2)}) async-start(s8[8388608]{0:T(1024)(128)(4,1)} %bitcast.237), calls=%async_computation.28 | async-start | bytes 8388608
  382.1 5.3 slice-start.5
  382.1 5.3 copy-start.14
  388.7 10.1 %copy-start.1 = (f32[8,512,512]{2,1,0:T(8,128)}, f32[8,512,512]{2,1,0:T(8,128)S(1)}, u32[]{:S(2)}) copy-start(f32[8,512,512]{2,1,0:T(8,128)S(1)} %add_add_fusion.2) | copy-start | bytes 25165828
  419.2 77.4 %reduce-scatter.21.cloned.1.call-start = ((), (), s32[]{:S(2)}) async-start(), calls=%async_computation.21 | async-start | bytes 5455872 | tf_op jit(solution)/shard_map/reduce_scatter | solution.py:66
  419.3 6.8 %copy-start.17 = (bf16[512,4672]{1,0:T(8,128)(2,1)S(1)}, bf16[512,4672]{1,0:T(8,128)(2,1)}, u32[]{:S(2)}) copy-start(bf16[512,4672]{1,0:T(8,128)(2,1)} %all-gather.21.cloned.1.call-done) | copy-start | bytes 14352388
  419.3 12.1 %slice-start.6 = ((s8[8388608]{0:T(1024)(128)(4,1)}), s8[4194304]{0:T(1024)(128)(4,1)S(1)}, s32[]{:S(2)}) async-start(s8[8388608]{0:T(1024)(128)(4,1)} %bitcast.239), calls=%async_computation.30 | async-start | bytes 8388608
  426.1 5.3 slice-start.7
  426.1 5.3 copy-start.12
  432.8 10.3 %copy-start = (f32[8,512,512]{2,1,0:T(8,128)}, f32[8,512,512]{2,1,0:T(8,128)S(1)}, u32[]{:S(2)}) copy-start(f32[8,512,512]{2,1,0:T(8,128)S(1)} %add_add_fusion) | copy-start | bytes 25165828
  463.2 34.8 %copy-start.8 = (f32[4672]{0:T(1024)S(1)}, f32[4672]{0:T(1024)}, u32[]{:S(2)}) copy-start(f32[4672]{0:T(1024)} %get-tuple-element.9) | copy-start | bytes 56068
  463.3 71.3 %all-gather.23.cloned.1.call-start = ((), (), s32[]{:S(2)}) async-start(), calls=%async_computation.22 | async-start | bytes 5455872 | tf_op jit(solution)/shard_map/all_gather | solution.py:70
  500.8 76.1 %all-gather.15.cloned.1.call-start = ((), (), s32[]{:S(2)}) async-start(), calls=%async_computation.14 | async-start | bytes 5455872 | tf_op jit(solution)/shard_map/all_gather | solution.py:70
  501.4 117.4 %reduce-scatter.23.cloned.1.call-start = ((), (), s32[]{:S(2)}) async-start(), calls=%async_computation.23 | async-start | bytes 5455872 | tf_op jit(solution)/shard_map/reduce_scatter | solution.py:75
  576.6 75.5 %reduce-scatter.15.cloned.1.call-start = ((), (), s32[]{:S(2)}) async-start(), calls=%async_computation.15 | async-start | bytes 5455872 | tf_op jit(solution)/shard_map/reduce_scatter | solution.py:75
  618.7 1.1 copy-start.6
  618.7 33.4 %copy-start.5 = (bf16[64,4672]{1,0:T(8,128)(2,1)S(1)}, bf16[64,4672]{1,0:T(8,128)(2,1)}, u32[]{:S(2)}) copy-start(bf16[64,4672]{1,0:T(8,128)(2,1)} %reduce-scatter.13.cloned.1.call-done) | copy-start | bytes 1794052
Sparse Core Ops, SparseCore 0:
  12.6 35.9 all-gather.8
  50.1 31.4 all-gather.16
  104.8 33.1 reduce-scatter.8
  149.0 33.1 reduce-scatter.16
  186.9 33.6 all-gather.10
  222.0 31.4 all-gather.18
  262.7 33.1 reduce-scatter.10
  304.8 33.1 reduce-scatter.18
  341.7 33.5 all-gather.12
  376.7 31.4 all-gather.20
  419.3 33.1 reduce-scatter.12
  463.4 33.1 reduce-scatter.20
  500.9 33.6 all-gather.22
  536.0 31.4 all-gather.14
  576.7 33.1 reduce-scatter.22
  618.9 33.1 reduce-scatter.14

commit v2 on v1

v2 whole, which is shorter than its diff:
```python
import functools

import jax
import jax.numpy as jnp
from jax import lax
from jax.experimental import pallas as pl
from jax.experimental.pallas import tpu as pltpu
from jax.sharding import PartitionSpec as P

MESH = pl.DeviceIdType.MESH
F32, BF16 = jnp.float32, jnp.bfloat16
TILE = 256
DUE = ((3, 3.5), (4, 8.0), (5, 14.0), (6, 17.5), (7, 21.5), (9, 24.5), (8, 27.5), (10, 31.0))
COST = {'qkv': 1.4, 'attn': 2.5, 'out': 0.75, 'pair': 2.8, 'rest': 1.5, 'down': 2.2}


def plan_steps(pieces):
    table, clock, left = {}, 0.0, list(DUE)
    for name, count in pieces:
        for index in range(count):
            clock += COST[name]
            while left and left[0][1] <= clock:
                table.setdefault((name, index), []).append(left.pop(0)[0])
    table['end'] = [step for step, _ in left]
    return table


def col_tiles(width):
    step = -(-width // (4 * TILE)) * TILE
    return [(start, min(step, width - start)) for start in range(0, width, step)]


def encoder_kernel(group, tokens, key_bias, table, norm_a, norm_m, w_query, w_key, w_value, w_out, w_act, w_lin, w_down,
                   out, h, part, sib, ring, qkv, ctx, gate, toep, wa_buf, wr_buf, wd_buf, wl_buf,
                   rs_send, rs_recv, ag_send, ag_recv, wa_sem, wr_sem, wd_sem, tok_sem):
    layers, dim, inner = w_query.shape
    heads = table.shape[0]
    ff = w_act.shape[2]
    chips = group // 2
    rows = tokens.shape[1]
    seq_len = rows * group
    chunk, half = rows // 2, rows // 4
    n_slot = 4 * layers
    qkv_refs = (w_query, w_key, w_value)
    per_ref = inner // TILE
    n_qkv = 3 * per_ref
    n_pair = ff // TILE
    rest = ff - n_pair * TILE
    tiles = col_tiles(dim)
    q_rows = 128

    me = lax.axis_index('tp')
    x, core = me // 2, me % 2
    right_x, left_x, far_x = (x + 1) % chips, (x + chips - 1) % chips, (x + 2) % chips
    right, left, sibling = right_x * 2 + core, left_x * 2 + core, x * 2 + (1 - core)

    def span(c):
        return pl.ds(c * chunk, chunk)

    def upper(c):
        return pl.ds(c * chunk, half)

    def lower(c):
        return pl.ds(c * chunk + half, half)

    def rs_copy(cs, c, event):
        if event == 6:
            src, dst, dev = part.at[cs, :, 1 - core, span(c)], sib.at[cs, :, span(c)], sibling
        else:
            block = (far_x, right_x, right_x, far_x, left_x, left_x)[event]
            piece = (upper, lower, upper, lower, upper, lower)[event](c)
            src, dst = part.at[cs, block, core, piece], ring.at[cs, event, c]
            dev = right if event < 3 else left
        return pltpu.make_async_remote_copy(src_ref=src, dst_ref=dst, send_sem=rs_send.at[cs, c, event],
                                            recv_sem=rs_recv.at[cs, c, event], device_id={'tp': dev}, device_id_type=MESH)

    def ag_copy(cs, c, event, arriving=False):
        piece = (upper, lower, upper, lower, upper, lower, span, span, span, span)[event](c)
        if arriving:
            block = (left_x, left_x, far_x, right_x, right_x, far_x, x, left_x, right_x, far_x)[event]
            lane = core if event < 6 else 1 - core
        else:
            block = (x, x, left_x, x, x, right_x, x, left_x, right_x, far_x)[event]
            lane = core
        ref = h.at[cs, block, lane, piece]
        dev = right if event < 3 else left if event < 6 else sibling
        return pltpu.make_async_remote_copy(src_ref=ref, dst_ref=ref, send_sem=ag_send.at[cs, c, event],
                                            recv_sem=ag_recv.at[cs, c, event], device_id={'tp': dev}, device_id_type=MESH)

    def arrived(cs, c, event):
        ag_copy(cs, c, event, arriving=True).wait_recv()

    def add_rows(cs, block, piece, other):
        part[cs, block, core, piece] = (part[cs, block, core, piece].astype(F32) + other.astype(F32)).astype(BF16)

    def rs_begin(cs):
        for c in range(2):
            rs_copy(cs, c, 6).start()

    def rs_local(cs, c):
        rs_copy(cs, c, 6).wait_recv()
        add_rows(cs, far_x, span(c), sib[cs, far_x, span(c)])
        rs_copy(cs, c, 0).start()
        rs_copy(cs, c, 3).start()
        add_rows(cs, right_x, span(c), sib[cs, right_x, span(c)])
        rs_copy(cs, c, 1).start()
        add_rows(cs, left_x, span(c), sib[cs, left_x, span(c)])
        rs_copy(cs, c, 4).start()

    def rs_pass(cs, c):
        rs_copy(cs, c, 0).wait_recv()
        add_rows(cs, right_x, upper(c), ring[cs, 0, c])
        rs_copy(cs, c, 2).start()
        rs_copy(cs, c, 3).wait_recv()
        add_rows(cs, left_x, lower(c), ring[cs, 3, c])
        rs_copy(cs, c, 5).start()

    def normalise(cs, c, gain):
        rows32 = out[cs, span(c)].astype(F32)
        inv_rms = lax.rsqrt(jnp.mean(rows32 * rows32, axis=-1, keepdims=True) + 1e-6)
        h[cs, x, core, span(c)] = (rows32 * inv_rms * gain).astype(BF16)

    def ag_begin(cs, c):
        for event in (0, 3, 1, 4, 6):
            ag_copy(cs, c, event).start()

    def gain_of(index):
        row = pl.ds(index // 2, 1)
        return jnp.where(index % 2 == 0, norm_a[row, :], norm_m[row, :])

    def rs_finish(cs, c):
        for event in (1, 2, 4, 5):
            rs_copy(cs, c, event).wait_recv()
        for piece, first, second in ((upper(c), 2, 4), (lower(c), 1, 5)):
            total = part[cs, x, core, piece].astype(F32) + sib[cs, x, piece].astype(F32)
            total = total + ring[cs, first, c].astype(F32) + ring[cs, second, c].astype(F32)
            out[cs, piece] = (out[cs, piece].astype(F32) + total).astype(BF16)

    def ag_forward(cs, c):
        arrived(cs, c, 0)
        ag_copy(cs, c, 2).start()
        arrived(cs, c, 3)
        ag_copy(cs, c, 5).start()

    def ag_share(cs, c):
        arrived(cs, c, 1)
        ag_copy(cs, c, 7).start()
        arrived(cs, c, 4)
        ag_copy(cs, c, 8).start()

    def ag_share_far(cs, c):
        arrived(cs, c, 2)
        arrived(cs, c, 5)
        ag_copy(cs, c, 9).start()

    def ag_end(cs):
        for c in range(2):
            for event in (6, 7, 8, 9):
                arrived(cs, c, event)
        for c in range(2):
            for event in range(10):
                ag_copy(cs, c, event).wait_send()

    def rs_end(cs):
        for c in range(2):
            for event in range(7):
                rs_copy(cs, c, event).wait_send()

    def step(number, slot):
        cs = (slot + 1) % 2
        c = 1 - number % 2 if number < 7 else 0 if number in (7, 9, 11) else 1
        if number in (3, 4):
            @pl.when(slot > 0)
            def _():
                rs_pass(cs, c)
        elif number in (5, 6):
            @pl.when(slot > 0)
            def _():
                rs_finish(cs, c)

                @pl.when(slot < n_slot - 1)
                def _():
                    normalise(cs, c, gain_of((slot + 1) // 2))
                    ag_begin(cs, c)
        else:
            @pl.when(slot < n_slot - 1)
            def _():
                (ag_forward if number in (7, 8) else ag_share if number in (9, 10) else ag_share_far)(cs, c)

    def phase_end(slot, left_over):
        for number in left_over:
            step(number, slot)
        rs_begin(slot % 2)
        rs_local(slot % 2, 0)
        rs_local(slot % 2, 1)
        step(11, slot)
        step(12, slot)

        @pl.when(slot > 0)
        def _():
            rs_end((slot + 1) % 2)

        @pl.when(slot < n_slot - 1)
        def _():
            ag_end((slot + 1) % 2)

    def run_steps(plan, name, index, slot):
        for (piece, at), numbers in [item for item in plan.items() if item[0] != 'end']:
            if piece != name:
                continue
            if isinstance(index, int):
                if index == at:
                    for number in numbers:
                        step(number, slot)
            else:
                @pl.when(index == at)
                def _():
                    for number in numbers:
                        step(number, slot)

    def load_qkv(layer, tile, slot):
        for index, ref in enumerate(qkv_refs):
            @pl.when(tile // per_ref == index)
            def _():
                cols = pl.ds(pl.multiple_of(tile % per_ref * TILE, TILE), TILE)
                pltpu.make_async_copy(ref.at[layer, :, cols], wa_buf.at[slot], wa_sem.at[slot]).start()

    def load_pair(layer, pair, slot):
        cols = pl.ds(pl.multiple_of(pair * TILE, TILE), TILE)
        for index, ref in enumerate((w_act, w_lin)):
            pltpu.make_async_copy(ref.at[layer, :, cols], wa_buf.at[slot + index], wa_sem.at[slot + index]).start()

    def wait_tile(slot):
        pltpu.make_async_copy(w_query.at[0, :, pl.ds(0, TILE)], wa_buf.at[slot], wa_sem.at[slot]).wait()

    def first_qkv(layer):
        for tile in range(min(4, n_qkv)):
            load_qkv(layer, tile, tile)

    def rest_copy(layer, index):
        ref = (w_act, w_lin)[index]
        return pltpu.make_async_copy(ref.at[layer, :, pl.ds(n_pair * TILE, rest)], wr_buf.at[index], wr_sem.at[index])

    def first_pairs(layer):
        for pair in range(min(2, n_pair)):
            load_pair(layer, pair, 2 * pair)
        for index in range(2):
            rest_copy(layer, index).start()

    def down_copy(ref, layer, tile):
        start, width = tiles[tile]
        depth = ref.shape[1]
        last = tile == len(tiles) - 1
        dst = wl_buf.at[pl.ds(0, depth)] if last else wd_buf.at[tile % 2, pl.ds(0, depth)]
        sem = wd_sem.at[2 if last else tile % 2]
        return pltpu.make_async_copy(ref.at[layer, :, pl.ds(start, width)], dst, sem)

    def down_begin(ref, layer):
        down_copy(ref, layer, len(tiles) - 1).start()
        for tile in range(min(2, len(tiles) - 1)):
            down_copy(ref, layer, tile).start()

    def down(ref, layer, seq, slot, left_ref, plan, name):
        depth = ref.shape[1]
        for tile, (start, width) in enumerate(tiles):
            down_copy(ref, layer, tile).wait()
            last = tile == len(tiles) - 1
            weight = wl_buf[pl.ds(0, depth)] if last else wd_buf[tile % 2, pl.ds(0, depth)]
            product = jnp.dot(left_ref[...], weight, preferred_element_type=F32).astype(BF16)
            part[seq, :, :, :, pl.ds(start, width)] = product.reshape(chips, 2, rows, width)
            if tile + 2 < len(tiles) - 1:
                down_copy(ref, layer, tile + 2).start()
            run_steps(plan, name, tile, slot)

    def gathered(seq):
        return h[seq].reshape(seq_len, dim)

    def attention_phase(layer, seq):
        slot = 4 * layer + seq
        plan = plan_steps((('qkv', n_qkv), ('attn', heads // 2), ('out', len(tiles))))
        down_begin(w_out, layer)

        def qkv_tile(tile, carry):
            buf = tile % 4
            wait_tile(buf)
            cols = pl.ds(pl.multiple_of(tile * TILE, TILE), TILE)
            qkv[:, cols] = jnp.dot(gathered(seq), wa_buf[buf], preferred_element_type=F32).astype(BF16)

            @pl.when(tile + 4 < n_qkv)
            def _():
                load_qkv(layer, tile + 4, buf)
            run_steps(plan, 'qkv', tile, slot)
            return carry
        lax.fori_loop(0, n_qkv, qkv_tile, 0)

        @pl.when(seq == 0)
        def _():
            first_qkv(layer)

        @pl.when(seq == 1)
        def _():
            first_pairs(layer)

        def head_pair(pair, carry):
            offset = pl.multiple_of(pair * 128, 128)
            keys = qkv[:, pl.ds(pl.multiple_of(inner + offset, 128), 128)]
            values = qkv[:, pl.ds(pl.multiple_of(2 * inner + offset, 128), 128)]
            mask_row = key_bias[seq]
            for block in range(seq_len // q_rows):
                queries = qkv[pl.ds(block * q_rows, q_rows), pl.ds(offset, 128)]
                lanes = lax.broadcasted_iota(jnp.int32, queries.shape, 1)
                mixed = []
                for side in range(2):
                    mine = jnp.where((lanes < 64) == (side == 0), queries, jnp.zeros_like(queries))
                    scores = lax.dot_general(mine, keys, (((1,), (1,)), ((), ())), preferred_element_type=F32)
                    bias = toep[2 * pair + side, :, pl.ds(seq_len - q_rows - block * q_rows, seq_len)]
                    scores = scores + bias + mask_row
                    weights = jnp.exp(scores - jnp.max(scores, axis=-1, keepdims=True))
                    probs = (weights * (1.0 / jnp.sum(weights, axis=-1, keepdims=True))).astype(BF16)
                    mixed.append(jnp.dot(probs, values, preferred_element_type=F32))
                ctx[pl.ds(block * q_rows, q_rows), pl.ds(offset, 128)] = jnp.where(lanes < 64, mixed[0], mixed[1]).astype(BF16)
            run_steps(plan, 'attn', pair, slot)
            return carry
        lax.fori_loop(0, heads // 2, head_pair, 0)

        down(w_out, layer, seq, slot, ctx, plan, 'out')
        phase_end(slot, plan['end'])

    def mlp_phase(layer, seq):
        slot = 4 * layer + 2 + seq
        plan = plan_steps((('pair', n_pair), ('rest', 1), ('down', len(tiles))))
        down_begin(w_down, layer)

        def pair_tile(pair, carry):
            buf = pair % 2 * 2
            wait_tile(buf)
            act = jnp.dot(gathered(seq), wa_buf[buf], preferred_element_type=F32)
            wait_tile(buf + 1)
            lin = jnp.dot(gathered(seq), wa_buf[buf + 1], preferred_element_type=F32)
            cols = pl.ds(pl.multiple_of(pair * TILE, TILE), TILE)
            gate[:, cols] = (jax.nn.gelu(act, approximate=True) * lin).astype(BF16)

            @pl.when(pair + 2 < n_pair)
            def _():
                load_pair(layer, pair + 2, buf)
            run_steps(plan, 'pair', pair, slot)
            return carry
        lax.fori_loop(0, n_pair, pair_tile, 0)

        for index in range(2):
            rest_copy(layer, index).wait()
        both = jnp.dot(gathered(seq), jnp.concatenate([wr_buf[0], wr_buf[1]], axis=1), preferred_element_type=F32)
        gate[:, n_pair * TILE:] = (jax.nn.gelu(both[:, :rest], approximate=True) * both[:, rest:]).astype(BF16)

        @pl.when(seq == 0)
        def _():
            first_pairs(layer)

        @pl.when((seq == 1) & (layer < layers - 1))
        def _():
            first_qkv(layer + 1)
        run_steps(plan, 'rest', 0, slot)
        down(w_down, layer, seq, slot, gate, plan, 'down')
        phase_end(slot, plan['end'])

    first_qkv(0)
    token_copy = pltpu.make_async_copy(tokens, out, tok_sem)
    token_copy.start()
    barrier = pltpu.get_barrier_semaphore()
    for device in (left, right, sibling):
        pl.semaphore_signal(barrier, inc=1, device_id={'tp': device}, device_id_type=MESH)
    pl.semaphore_wait(barrier, 3)
    token_copy.wait()

    for c in range(2):
        normalise(0, c, norm_a[pl.ds(0, 1), :])
        ag_begin(0, c)
    for c in range(2):
        normalise(1, c, norm_a[pl.ds(0, 1), :])

    offsets = lax.broadcasted_iota(jnp.int32, (heads, 2 * seq_len), 1) - (seq_len - 1)
    distance = jnp.minimum(jnp.abs(offsets), 128)
    bucket = jnp.full_like(distance, 8)
    for power in range(1, 8):
        bucket = bucket + (distance * distance >= 64 * 2 ** power).astype(jnp.int32)
    bucket = jnp.where(distance < 8, distance, bucket) + jnp.where(offsets > 0, 16, 0)
    values = jnp.zeros((heads, 2 * seq_len), F32)
    for index in range(table.shape[1]):
        values = jnp.where(bucket == index, table[:, index:index + 1], values)
    for head in range(heads):
        wide = jnp.broadcast_to(values[head:head + 1], (q_rows, 2 * seq_len))
        toep[head] = pltpu.roll(wide, 2 * seq_len - (q_rows - 1), 1, stride=1, stride_axis=0)[:, :2 * seq_len - q_rows]

    for c in range(2):
        ag_forward(0, c)
    for c in range(2):
        ag_begin(1, c)
    for c in range(2):
        ag_share(0, c)
    for c in range(2):
        ag_share_far(0, c)
    ag_end(0)

    def layer_body(layer, carry):
        for phase in (attention_phase, mlp_phase):
            def one(seq, inner_carry):
                phase(layer, seq)
                return inner_carry
            lax.fori_loop(0, 2, one, 0)
        return carry
    lax.fori_loop(0, layers, layer_body, 0)

    for c in range(2):
        rs_pass(1, c)
    for c in range(2):
        rs_finish(1, c)
    rs_end(1)


def solution(mesh):
    group = mesh.shape['tp']
    col_spec = P(None, None, 'tp')
    row_spec = P(None, 'tp', None)

    def local_fn(tokens, pad_mask, rel_table, w_query, w_key, w_value, w_out, w_act, w_lin, w_down, norm_attn, norm_mlp):
        batch, rows, dim = tokens.shape
        seq_len = rows * group
        heads, inner, ff = rel_table.shape[1], w_query.shape[2], w_act.shape[2]
        rest = ff % TILE
        tiles = col_tiles(dim)
        key_bias = jnp.where(pad_mask == 1, 0.0, -1e9).astype(F32)[:, None, :]
        vmem, hbm = pl.BlockSpec(memory_space=pltpu.VMEM), pl.BlockSpec(memory_space=pl.ANY)
        return pl.pallas_call(
            functools.partial(encoder_kernel, group),
            out_shape=jax.ShapeDtypeStruct(tokens.shape, BF16),
            in_specs=[hbm, vmem, vmem, vmem, vmem] + [hbm] * 7,
            out_specs=vmem,
            scratch_shapes=[
                pltpu.VMEM((batch, group // 2, 2, rows, dim), BF16),
                pltpu.VMEM((batch, group // 2, 2, rows, dim), BF16),
                pltpu.VMEM((2, group // 2, rows, dim), BF16),
                pltpu.VMEM((2, 6, 2, rows // 4, dim), BF16),
                pltpu.VMEM((seq_len, 3 * inner), BF16),
                pltpu.VMEM((seq_len, inner), BF16),
                pltpu.VMEM((seq_len, ff), BF16),
                pltpu.VMEM((heads, 128, 2 * seq_len - 128), F32),
                pltpu.VMEM((4, dim, TILE), BF16),
                pltpu.VMEM((2, dim, rest), BF16),
                pltpu.VMEM((2, ff, tiles[0][1]), BF16),
                pltpu.VMEM((ff, tiles[-1][1]), BF16),
                pltpu.SemaphoreType.DMA((2, 2, 7)),
                pltpu.SemaphoreType.DMA((2, 2, 7)),
                pltpu.SemaphoreType.DMA((2, 2, 10)),
                pltpu.SemaphoreType.DMA((2, 2, 10)),
                pltpu.SemaphoreType.DMA((4,)),
                pltpu.SemaphoreType.DMA((2,)),
                pltpu.SemaphoreType.DMA((3,)),
                pltpu.SemaphoreType.DMA,
            ],
            compiler_params=pltpu.CompilerParams(collective_id=0, has_side_effects=True, vmem_limit_bytes=67_000_000),
            name='encoder',
        )(tokens, key_bias, rel_table.T, norm_attn, norm_mlp, w_query, w_key, w_value, w_out, w_act, w_lin, w_down)

    in_specs = (P('dp', 'tp', None), P('dp', None), P(None, 'tp'), col_spec, col_spec, col_spec, row_spec,
                col_spec, col_spec, row_spec, P(None, None), P(None, None))
    return jax.shard_map(local_fn, mesh=mesh, in_specs=in_specs, out_specs=P('dp', 'tp', None), check_vma=False)
```

time: 673 us -> 537 us (0.80); the launches traced: 661 us -> 534 us
  Pallas kernels: 5.18 us -> 435 us
  matrix products: 342 us -> 0 us
  waiting for transfers between devices: 260 us -> 0 us
  local copies, waits for them, and re-layouts: 3.95 us -> 98.8 us
  other arithmetic: 34.3 us -> 0.69 us
  between operations: 14.2 us -> 0.01 us
    pallas_call x1, Pallas kernels: 5.18 us -> 435 us  [local_fn(): pl.pallas_call(functools.partial(encoder_kernel, group), out_shape=jax.Sh...]
    dot_general x32 -> x0, matrix products: 342 us -> none  [the longest x4 110 us: local_fn(): jnp.dot(gated, w_down[layer_idx], preferred_element_type=jnp.float32)]
    all_gather x8 -> x0, waiting for transfers between devices: 129 us -> none  [the longest x4 66.2 us: local_fn(): lax.all_gather(rms_norm(residual, norm_mlp[layer_idx]), 'tp', axis=0, til...]
    reduce_scatter x8 -> x0, waiting for transfers between devices: 128 us -> none  [the longest x4 64.3 us: local_fn(): ffn_out = lax.psum_scatter(part_out, 'tp', scatter_dimension=0, tiled=True)]
    unnamed x56 -> x4, local copies, waits for them, and re-layouts: 1.72 us -> 98.2 us
    sub x4 -> x0, other arithmetic: 12.8 us -> none  [local_fn(): jax.nn.softmax(scores + rel_bias + key_bias[row], axis=-1)]
    convert_element_type x4 -> x0, other arithmetic: 9.49 us -> none  [rms_norm(): return (rows32 * inv_rms * gain_vec).astype(jnp.bfloat16)]
    reduce_sum x5 -> x0, other arithmetic: 8.19 us -> none  [rms_norm(): jnp.mean(rows32 * rows32, axis=-1, keepdims=True) + 1e-06]
  transfers between devices with their start and end apart: 16 -> 0, of which waited for: 8 -> 0; matrix products, arithmetic and copies ran while one was open for 54% -> 0% of each run, Pallas kernels for 1% -> 0%
where the time goes in v2:
time: 537 us; the launch traced here: 534 us
  Pallas kernels  435 us (81%)
  local copies, waits for them, and re-layouts  98.8 us (18%)
    pallas_call x1, Pallas kernels, local_fn(): pl.pallas_call(functools.partial(encoder_kernel, group), out_shape=jax.Sh...  435 us
    unnamed x4, local copies, waits for them, and re-layouts  98.2 us

profile of v2, /device:TPU:81, one launch (start us, length us, event | category | flops | bytes accessed | tf_op | source)
XLA Modules:
  0.0 534.4 jit_solution(13864555286048193477)
XLA Ops:
  0.0 0.7 compare_select_fusion
  0.7 0.6 broadcast_in_dim.13.key_bias
  1.3 12.9 %copy.13.w_out = bf16[2,512,4672]{2,1,0:T(8,128)(2,1)} copy(bf16[2,512,4672]{1,2,0:T(8,128)(2,1)} %param.18) | data formatting | bytes 19136512 | tf_op args[6]
  14.2 41.6 %copy.14.w_act = bf16[2,4672,1544]{2,1,0:T(8,128)(2,1)} copy(bf16[2,4672,1544]{1,2,0:T(8,128)(2,1)} %param.19) | data formatting | bytes 57708544 | tf_op args[7]
  55.8 41.3 %copy.15.w_lin = bf16[2,4672,1544]{2,1,0:T(8,128)(2,1)} copy(bf16[2,4672,1544]{1,2,0:T(8,128)(2,1)} %param.20) | data formatting | bytes 57708544 | tf_op args[8]
  97.1 434.9 %encoder.1 = bf16[2,64,4672]{2,1,0:T(8,128)(2,1)} custom-call(bf16[2,64,4672]{2,1,0:T(8,128)(2,1)} %tokens.1, f32[2,1,512]{2,1,0:T(1,128)} %broadcast_in_dim.13.key_bias, f32[8,32]{1,0:T(8,128)} %bitcast.1, f32[2,4672]{1,0:T(2,128)} %norm_a.1, f32[2,4672]{1,0:T(2,128)} %norm_m.1, bf16[2,4672,512]{2,1,0:T(8,128)(2,1)} %w_query.1, ...), custom_call_target="tpu_custom_call" | custom-call | tf_op jit(solution)/shard_map/encoder/pallas_call | solution.py:433
  532.0 2.4 copy.17

commit v3 on v2

--- a/solution.py
+++ b/solution.py
@@ -10,43 +10,50 @@
 MESH = pl.DeviceIdType.MESH
 F32, BF16 = jnp.float32, jnp.bfloat16
 TILE = 256
-DUE = ((3, 3.5), (4, 8.0), (5, 14.0), (6, 17.5), (7, 21.5), (9, 24.5), (8, 27.5), (10, 31.0))
-COST = {'qkv': 1.4, 'attn': 2.5, 'out': 0.75, 'pair': 2.8, 'rest': 1.5, 'down': 2.2}
-
-
-def plan_steps(pieces):
-    table, clock, left = {}, 0.0, list(DUE)
+N_CHUNK = 2
+DUE = {1: (('pass', 0, 8.0), ('finish', 0, 19.0), ('forward', 0, 27.0), ('share', 0, 33.0)),
+       2: (('pass', 0, 3.5), ('pass', 1, 8.0), ('finish', 0, 14.0), ('finish', 1, 17.5),
+           ('forward', 0, 21.5), ('share', 0, 24.5), ('forward', 1, 27.5), ('share', 1, 31.0))}
+COST = {'qkv': 1.9, 'attn': 3.5, 'out': 1.3, 'pair': 2.1, 'rest': 2.2, 'down': 2.1}
+
+
+def plan_steps(pieces, n_chunk):
+    table, clock, left = {}, 0.0, list(DUE[n_chunk])
     for name, count in pieces:
         for index in range(count):
             clock += COST[name]
-            while left and left[0][1] <= clock:
-                table.setdefault((name, index), []).append(left.pop(0)[0])
-    table['end'] = [step for step, _ in left]
+            while left and left[0][2] <= clock:
+                table.setdefault((name, index), []).append(left.pop(0)[:2])
+    table['end'] = [item[:2] for item in left]
     return table
 
 
-def col_tiles(width):
-    step = -(-width // (4 * TILE)) * TILE
-    return [(start, min(step, width - start)) for start in range(0, width, step)]
-
-
-def encoder_kernel(group, tokens, key_bias, table, norm_a, norm_m, w_query, w_key, w_value, w_out, w_act, w_lin, w_down,
-                   out, h, part, sib, ring, qkv, ctx, gate, toep, wa_buf, wr_buf, wd_buf, wl_buf,
-                   rs_send, rs_recv, ag_send, ag_recv, wa_sem, wr_sem, wd_sem, tok_sem):
+def col_tiles(width, pieces):
+    step = -(-width // (pieces * TILE)) * TILE
+    starts = list(range(0, width, step))
+    if len(starts) > 1 and width - starts[-1] <= TILE // 2:
+        starts.pop()
+    return [(start, end - start) for start, end in zip(starts, starts[1:] + [width])]
+
+
+def encoder_kernel(group, n_chunk, tokens, pad_mask, table, norm_a, norm_m, w_query, w_key, w_value, w_out, w_act, w_lin, w_down,
+                   out, h, part, sib, ring, qkv, ctx, gate, toep, wq_buf, wa_buf, wr_buf, wo_buf, wd_buf, wl_buf,
+                   rs_send, rs_recv, ag_send, ag_recv, wq_sem, wa_sem, wr_sem, wo_sem, wd_sem, tok_sem):
     layers, dim, inner = w_query.shape
     heads = table.shape[0]
-    ff = w_act.shape[2]
+    ff = w_act.shape[1]
     chips = group // 2
     rows = tokens.shape[1]
     seq_len = rows * group
-    chunk, half = rows // 2, rows // 4
+    chunk, half = rows // n_chunk, rows // n_chunk // 2
     n_slot = 4 * layers
     qkv_refs = (w_query, w_key, w_value)
     per_ref = inner // TILE
     n_qkv = 3 * per_ref
     n_pair = ff // TILE
     rest = ff - n_pair * TILE
-    tiles = col_tiles(dim)
+    out_tiles, tiles = col_tiles(dim, 4), col_tiles(dim, 6)
+    n_wq = wq_buf.shape[0]
     q_rows = 128
 
     me = lax.axis_index('tp')
@@ -94,7 +101,7 @@
         part[cs, block, core, piece] = (part[cs, block, core, piece].astype(F32) + other.astype(F32)).astype(BF16)
 
     def rs_begin(cs):
-        for c in range(2):
+        for c in range(n_chunk):
             rs_copy(cs, c, 6).start()
 
     def rs_local(cs, c):
@@ -154,26 +161,26 @@
         ag_copy(cs, c, 9).start()
 
     def ag_end(cs):
-        for c in range(2):
+        for c in range(n_chunk):
             for event in (6, 7, 8, 9):
                 arrived(cs, c, event)
-        for c in range(2):
+        for c in range(n_chunk):
             for event in range(10):
                 ag_copy(cs, c, event).wait_send()
 
     def rs_end(cs):
-        for c in range(2):
+        for c in range(n_chunk):
             for event in range(7):
                 rs_copy(cs, c, event).wait_send()
 
-    def step(number, slot):
+    def step(item, slot):
+        name, c = item
         cs = (slot + 1) % 2
-        c = 1 - number % 2 if number < 7 else 0 if number in (7, 9, 11) else 1
-        if number in (3, 4):
+        if name == 'pass':
             @pl.when(slot > 0)
             def _():
                 rs_pass(cs, c)
-        elif number in (5, 6):
+        elif name == 'finish':
             @pl.when(slot > 0)
             def _():
                 rs_finish(cs, c)
@@ -185,16 +192,16 @@
         else:
             @pl.when(slot < n_slot - 1)
             def _():
-                (ag_forward if number in (7, 8) else ag_share if number in (9, 10) else ag_share_far)(cs, c)
+                {'forward': ag_forward, 'share': ag_share, 'far': ag_share_far}[name](cs, c)
 
     def phase_end(slot, left_over):
-        for number in left_over:
-            step(number, slot)
         rs_begin(slot % 2)
-        rs_local(slot % 2, 0)
-        rs_local(slot % 2, 1)
-        step(11, slot)
-        step(12, slot)
+        for item in left_over:
+            step(item, slot)
+        for c in range(n_chunk):
+            rs_local(slot % 2, c)
+        for c in range(n_chunk):
+            step(('far', c), slot)
 
         @pl.when(slot > 0)
         def _():
@@ -205,41 +212,44 @@
             ag_end((slot + 1) % 2)
 
     def run_steps(plan, name, index, slot):
-        for (piece, at), numbers in [item for item in plan.items() if item[0] != 'end']:
+        for (piece, at), items in [entry for entry in plan.items() if entry[0] != 'end']:
             if piece != name:
                 continue
             if isinstance(index, int):
                 if index == at:
-                    for number in numbers:
-                        step(number, slot)
+                    for item in items:
+                        step(item, slot)
             else:
                 @pl.when(index == at)
                 def _():
-                    for number in numbers:
-                        step(number, slot)
+                    for item in items:
+                        step(item, slot)
 
     def load_qkv(layer, tile, slot):
         for index, ref in enumerate(qkv_refs):
             @pl.when(tile // per_ref == index)
             def _():
                 cols = pl.ds(pl.multiple_of(tile % per_ref * TILE, TILE), TILE)
-                pltpu.make_async_copy(ref.at[layer, :, cols], wa_buf.at[slot], wa_sem.at[slot]).start()
+                pltpu.make_async_copy(ref.at[layer, :, cols], wq_buf.at[slot], wq_sem.at[slot]).start()
 
     def load_pair(layer, pair, slot):
         cols = pl.ds(pl.multiple_of(pair * TILE, TILE), TILE)
         for index, ref in enumerate((w_act, w_lin)):
-            pltpu.make_async_copy(ref.at[layer, :, cols], wa_buf.at[slot + index], wa_sem.at[slot + index]).start()
+            pltpu.make_async_copy(ref.at[layer, cols, :], wa_buf.at[slot + index], wa_sem.at[slot + index]).start()
 
     def wait_tile(slot):
-        pltpu.make_async_copy(w_query.at[0, :, pl.ds(0, TILE)], wa_buf.at[slot], wa_sem.at[slot]).wait()
+        pltpu.make_async_copy(w_act.at[0, pl.ds(0, TILE), :], wa_buf.at[slot], wa_sem.at[slot]).wait()
+
+    def wait_qkv(slot):
+        pltpu.make_async_copy(w_query.at[0, :, pl.ds(0, TILE)], wq_buf.at[slot], wq_sem.at[slot]).wait()
 
     def first_qkv(layer):
-        for tile in range(min(4, n_qkv)):
+        for tile in range(min(n_wq, n_qkv)):
             load_qkv(layer, tile, tile)
 
     def rest_copy(layer, index):
         ref = (w_act, w_lin)[index]
-        return pltpu.make_async_copy(ref.at[layer, :, pl.ds(n_pair * TILE, rest)], wr_buf.at[index], wr_sem.at[index])
+        return pltpu.make_async_copy(ref.at[layer, pl.ds(n_pair * TILE, rest), :], wr_buf.at[index], wr_sem.at[index])
 
     def first_pairs(layer):
         for pair in range(min(2, n_pair)):
@@ -247,48 +257,41 @@
         for index in range(2):
             rest_copy(layer, index).start()
 
-    def down_copy(ref, layer, tile):
+    def out_copy(layer, tile):
+        start, width = out_tiles[tile]
+        return pltpu.make_async_copy(w_out.at[layer, pl.ds(start, width), :], wo_buf.at[tile % 2, pl.ds(0, width)],
+                                     wo_sem.at[tile % 2])
+
+    def down_copy(layer, tile):
         start, width = tiles[tile]
-        depth = ref.shape[1]
         last = tile == len(tiles) - 1
-        dst = wl_buf.at[pl.ds(0, depth)] if last else wd_buf.at[tile % 2, pl.ds(0, depth)]
-        sem = wd_sem.at[2 if last else tile % 2]
-        return pltpu.make_async_copy(ref.at[layer, :, pl.ds(start, width)], dst, sem)
-
-    def down_begin(ref, layer):
-        down_copy(ref, layer, len(tiles) - 1).start()
-        for tile in range(min(2, len(tiles) - 1)):
-            down_copy(ref, layer, tile).start()
-
-    def down(ref, layer, seq, slot, left_ref, plan, name):
-        depth = ref.shape[1]
-        for tile, (start, width) in enumerate(tiles):
-            down_copy(ref, layer, tile).wait()
-            last = tile == len(tiles) - 1
-            weight = wl_buf[pl.ds(0, depth)] if last else wd_buf[tile % 2, pl.ds(0, depth)]
-            product = jnp.dot(left_ref[...], weight, preferred_element_type=F32).astype(BF16)
-            part[seq, :, :, :, pl.ds(start, width)] = product.reshape(chips, 2, rows, width)
-            if tile + 2 < len(tiles) - 1:
-                down_copy(ref, layer, tile + 2).start()
-            run_steps(plan, name, tile, slot)
+        dst = wl_buf if last else wd_buf.at[tile % 2]
+        return pltpu.make_async_copy(w_down.at[layer, :, pl.ds(start, width)], dst, wd_sem.at[2 if last else tile % 2])
+
+    def keep(seq, start, width, product):
+        part[seq, :, :, :, pl.ds(start, width)] = product.astype(BF16).reshape(chips, 2, rows, width)
+
+    def times_rows(left, right):
+        return lax.dot_general(left, right, (((1,), (1,)), ((), ())), preferred_element_type=F32)
 
     def gathered(seq):
         return h[seq].reshape(seq_len, dim)
 
     def attention_phase(layer, seq):
         slot = 4 * layer + seq
-        plan = plan_steps((('qkv', n_qkv), ('attn', heads // 2), ('out', len(tiles))))
-        down_begin(w_out, layer)
+        plan = plan_steps((('qkv', n_qkv), ('attn', heads // 2), ('out', len(out_tiles))), n_chunk)
+        for tile in range(min(2, len(out_tiles))):
+            out_copy(layer, tile).start()
 
         def qkv_tile(tile, carry):
-            buf = tile % 4
-            wait_tile(buf)
+            buf = tile % n_wq
+            wait_qkv(buf)
             cols = pl.ds(pl.multiple_of(tile * TILE, TILE), TILE)
-            qkv[:, cols] = jnp.dot(gathered(seq), wa_buf[buf], preferred_element_type=F32).astype(BF16)
-
-            @pl.when(tile + 4 < n_qkv)
-            def _():
-                load_qkv(layer, tile + 4, buf)
+            qkv[:, cols] = jnp.dot(gathered(seq), wq_buf[buf], preferred_element_type=F32).astype(BF16)
+
+            @pl.when(tile + n_wq < n_qkv)
+            def _():
+                load_qkv(layer, tile + n_wq, buf)
             run_steps(plan, 'qkv', tile, slot)
             return carry
         lax.fori_loop(0, n_qkv, qkv_tile, 0)
@@ -305,7 +308,7 @@
             offset = pl.multiple_of(pair * 128, 128)
             keys = qkv[:, pl.ds(pl.multiple_of(inner + offset, 128), 128)]
             values = qkv[:, pl.ds(pl.multiple_of(2 * inner + offset, 128), 128)]
-            mask_row = key_bias[seq]
+            mask_row = jnp.where(pad_mask[pl.ds(seq, 1), :] == 1, 0.0, -1e9).astype(F32)
             for block in range(seq_len // q_rows):
                 queries = qkv[pl.ds(block * q_rows, q_rows), pl.ds(offset, 128)]
                 lanes = lax.broadcasted_iota(jnp.int32, queries.shape, 1)
@@ -323,33 +326,41 @@
             return carry
         lax.fori_loop(0, heads // 2, head_pair, 0)
 
-        down(w_out, layer, seq, slot, ctx, plan, 'out')
+        for tile, (start, width) in enumerate(out_tiles):
+            out_copy(layer, tile).wait()
+            keep(seq, start, width, times_rows(ctx[...], wo_buf[tile % 2, pl.ds(0, width)]))
+            if tile + 2 < len(out_tiles):
+                out_copy(layer, tile + 2).start()
+            run_steps(plan, 'out', tile, slot)
         phase_end(slot, plan['end'])
 
     def mlp_phase(layer, seq):
         slot = 4 * layer + 2 + seq
-        plan = plan_steps((('pair', n_pair), ('rest', 1), ('down', len(tiles))))
-        down_begin(w_down, layer)
+        plan = plan_steps((('pair', 2 * n_pair), ('rest', 1), ('down', len(tiles))), n_chunk)
+        down_copy(layer, len(tiles) - 1).start()
+        for tile in range(min(2, len(tiles) - 1)):
+            down_copy(layer, tile).start()
 
         def pair_tile(pair, carry):
             buf = pair % 2 * 2
             wait_tile(buf)
-            act = jnp.dot(gathered(seq), wa_buf[buf], preferred_element_type=F32)
+            act = times_rows(gathered(seq), wa_buf[buf])
+            run_steps(plan, 'pair', 2 * pair, slot)
             wait_tile(buf + 1)
-            lin = jnp.dot(gathered(seq), wa_buf[buf + 1], preferred_element_type=F32)
+            lin = times_rows(gathered(seq), wa_buf[buf + 1])
             cols = pl.ds(pl.multiple_of(pair * TILE, TILE), TILE)
             gate[:, cols] = (jax.nn.gelu(act, approximate=True) * lin).astype(BF16)
 
             @pl.when(pair + 2 < n_pair)
             def _():
                 load_pair(layer, pair + 2, buf)
-            run_steps(plan, 'pair', pair, slot)
+            run_steps(plan, 'pair', 2 * pair + 1, slot)
             return carry
         lax.fori_loop(0, n_pair, pair_tile, 0)
 
         for index in range(2):
             rest_copy(layer, index).wait()
-        both = jnp.dot(gathered(seq), jnp.concatenate([wr_buf[0], wr_buf[1]], axis=1), preferred_element_type=F32)
+        both = times_rows(gathered(seq), jnp.concatenate([wr_buf[0], wr_buf[1]], axis=0))
         gate[:, n_pair * TILE:] = (jax.nn.gelu(both[:, :rest], approximate=True) * both[:, rest:]).astype(BF16)
 
         @pl.when(seq == 0)
@@ -360,7 +371,13 @@
         def _():
             first_qkv(layer + 1)
         run_steps(plan, 'rest', 0, slot)
-        down(w_down, layer, seq, slot, gate, plan, 'down')
+        for tile, (start, width) in enumerate(tiles):
+            down_copy(layer, tile).wait()
+            weight = wl_buf[...] if tile == len(tiles) - 1 else wd_buf[tile % 2]
+            keep(seq, start, width, jnp.dot(gate[...], weight, preferred_element_type=F32))
+            if tile + 2 < len(tiles) - 1:
+                down_copy(layer, tile + 2).start()
+            run_steps(plan, 'down', tile, slot)
         phase_end(slot, plan['end'])
 
     first_qkv(0)
@@ -372,10 +389,10 @@
     pl.semaphore_wait(barrier, 3)
     token_copy.wait()
 
-    for c in range(2):
+    for c in range(n_chunk):
         normalise(0, c, norm_a[pl.ds(0, 1), :])
         ag_begin(0, c)
-    for c in range(2):
+    for c in range(n_chunk):
         normalise(1, c, norm_a[pl.ds(0, 1), :])
 
     offsets = lax.broadcasted_iota(jnp.int32, (heads, 2 * seq_len), 1) - (seq_len - 1)
@@ -391,13 +408,13 @@
         wide = jnp.broadcast_to(values[head:head + 1], (q_rows, 2 * seq_len))
         toep[head] = pltpu.roll(wide, 2 * seq_len - (q_rows - 1), 1, stride=1, stride_axis=0)[:, :2 * seq_len - q_rows]
 
-    for c in range(2):
+    for c in range(n_chunk):
         ag_forward(0, c)
-    for c in range(2):
+    for c in range(n_chunk):
         ag_begin(1, c)
-    for c in range(2):
+    for c in range(n_chunk):
         ag_share(0, c)
-    for c in range(2):
+    for c in range(n_chunk):
         ag_share_far(0, c)
     ag_end(0)
 
@@ -410,9 +427,9 @@
         return carry
     lax.fori_loop(0, layers, layer_body, 0)
 
-    for c in range(2):
+    for c in range(n_chunk):
         rs_pass(1, c)
-    for c in range(2):
+    for c in range(n_chunk):
         rs_finish(1, c)
     rs_end(1)
 
@@ -427,11 +444,10 @@
         seq_len = rows * group
         heads, inner, ff = rel_table.shape[1], w_query.shape[2], w_act.shape[2]
         rest = ff % TILE
-        tiles = col_tiles(dim)
-        key_bias = jnp.where(pad_mask == 1, 0.0, -1e9).astype(F32)[:, None, :]
+        out_tiles, tiles = col_tiles(dim, 4), col_tiles(dim, 6)
         vmem, hbm = pl.BlockSpec(memory_space=pltpu.VMEM), pl.BlockSpec(memory_space=pl.ANY)
         return pl.pallas_call(
-            functools.partial(encoder_kernel, group),
+            functools.partial(encoder_kernel, group, N_CHUNK),
             out_shape=jax.ShapeDtypeStruct(tokens.shape, BF16),
             in_specs=[hbm, vmem, vmem, vmem, vmem] + [hbm] * 7,
             out_specs=vmem,
@@ -439,27 +455,32 @@
                 pltpu.VMEM((batch, group // 2, 2, rows, dim), BF16),
                 pltpu.VMEM((batch, group // 2, 2, rows, dim), BF16),
                 pltpu.VMEM((2, group // 2, rows, dim), BF16),
-                pltpu.VMEM((2, 6, 2, rows // 4, dim), BF16),
+                pltpu.VMEM((2, 6, N_CHUNK, rows // N_CHUNK // 2, dim), BF16),
                 pltpu.VMEM((seq_len, 3 * inner), BF16),
                 pltpu.VMEM((seq_len, inner), BF16),
                 pltpu.VMEM((seq_len, ff), BF16),
                 pltpu.VMEM((heads, 128, 2 * seq_len - 128), F32),
-                pltpu.VMEM((4, dim, TILE), BF16),
-                pltpu.VMEM((2, dim, rest), BF16),
+                pltpu.VMEM((2, dim, TILE), BF16),
+                pltpu.VMEM((4, TILE, dim), BF16),
+                pltpu.VMEM((2, rest, dim), BF16),
+                pltpu.VMEM((2, out_tiles[0][1], inner), BF16),
                 pltpu.VMEM((2, ff, tiles[0][1]), BF16),
                 pltpu.VMEM((ff, tiles[-1][1]), BF16),
-                pltpu.SemaphoreType.DMA((2, 2, 7)),
-                pltpu.SemaphoreType.DMA((2, 2, 7)),
-                pltpu.SemaphoreType.DMA((2, 2, 10)),
-                pltpu.SemaphoreType.DMA((2, 2, 10)),
+                pltpu.SemaphoreType.DMA((2, N_CHUNK, 7)),
+                pltpu.SemaphoreType.DMA((2, N_CHUNK, 7)),
+                pltpu.SemaphoreType.DMA((2, N_CHUNK, 10)),
+                pltpu.SemaphoreType.DMA((2, N_CHUNK, 10)),
+                pltpu.SemaphoreType.DMA((2,)),
                 pltpu.SemaphoreType.DMA((4,)),
+                pltpu.SemaphoreType.DMA((2,)),
                 pltpu.SemaphoreType.DMA((2,)),
                 pltpu.SemaphoreType.DMA((3,)),
                 pltpu.SemaphoreType.DMA,
             ],
             compiler_params=pltpu.CompilerParams(collective_id=0, has_side_effects=True, vmem_limit_bytes=67_000_000),
             name='encoder',
-        )(tokens, key_bias, rel_table.T, norm_attn, norm_mlp, w_query, w_key, w_value, w_out, w_act, w_lin, w_down)
+        )(tokens, pad_mask, rel_table.T, norm_attn, norm_mlp, w_query, w_key, w_value, w_out.swapaxes(1, 2),
+          w_act.swapaxes(1, 2), w_lin.swapaxes(1, 2), w_down)
 
     in_specs = (P('dp', 'tp', None), P('dp', None), P(None, 'tp'), col_spec, col_spec, col_spec, row_spec,
                 col_spec, col_spec, row_spec, P(None, None), P(None, None))

time: 537 us -> 421 us (0.78)
  local copies, waits for them, and re-layouts: 98.8 us -> 2.39 us
  Pallas kernels: 435 us -> 418 us
    unnamed x4 -> x1, local copies, waits for them, and re-layouts: 98.2 us -> 2.39 us
    pallas_call x1, Pallas kernels: 435 us -> 418 us  [local_fn(): pl.pallas_call(functools.partial(encoder_kernel, group, N_CHUNK), out_sha...]
where the time goes in v3:
time: 421 us
  Pallas kernels  418 us (99%)
    pallas_call x1, Pallas kernels, local_fn(): pl.pallas_call(functools.partial(encoder_kernel, group, N_CHUNK), out_sha...  418 us

profile of v3, /device:TPU:81, one launch (start us, length us, event | category | flops | bytes accessed | tf_op | source)
XLA Modules:
  0.0 420.7 jit_solution(10777279278568918581)
XLA Ops:
  0.0 418.3 %encoder.1 = bf16[2,64,4672]{2,1,0:T(8,128)(2,1)} custom-call(bf16[2,64,4672]{2,1,0:T(8,128)(2,1)} %tokens.1, s32[2,512]{1,0:T(2,128)} %pad_mask.1, f32[8,32]{1,0:T(8,128)} %bitcast.7, f32[2,4672]{1,0:T(2,128)} %norm_a.1, f32[2,4672]{1,0:T(2,128)} %norm_m.1, bf16[2,4672,512]{2,1,0:T(8,128)(2,1)} %w_query.1, bf16[2,4672,512]{2,1,0:T(8,128)(2,1)} %w_key.1, ...), custom_call_target="tpu_custom_call" | custom-call | tf_op jit(solution)/shard_map/encoder/pallas_call | solution.py:449
  418.3 2.4 copy.14

commit v4 on v3

--- a/solution.py
+++ b/solution.py
@@ -13,7 +13,8 @@
 N_CHUNK = 2
 DUE = {1: (('pass', 0, 8.0), ('finish', 0, 19.0), ('forward', 0, 27.0), ('share', 0, 33.0)),
        2: (('pass', 0, 3.5), ('pass', 1, 8.0), ('finish', 0, 14.0), ('finish', 1, 17.5),
-           ('forward', 0, 21.5), ('share', 0, 24.5), ('forward', 1, 27.5), ('share', 1, 31.0))}
+           ('forward', 0, 21.5), ('share', 0, 24.5), ('forward', 1, 27.5), ('share', 1, 31.0), ('far', 0, 33.5),
+           ('far', 1, 35.5))}
 COST = {'qkv': 1.9, 'attn': 3.5, 'out': 1.3, 'pair': 2.1, 'rest': 2.2, 'down': 2.1}
 
 
@@ -197,11 +198,13 @@
     def phase_end(slot, left_over):
         rs_begin(slot % 2)
         for item in left_over:
-            step(item, slot)
+            if item[0] != 'far':
+                step(item, slot)
         for c in range(n_chunk):
             rs_local(slot % 2, c)
-        for c in range(n_chunk):
-            step(('far', c), slot)
+        for item in left_over:
+            if item[0] == 'far':
+                step(item, slot)
 
         @pl.when(slot > 0)
         def _():

time: 421 us -> 419 us (level)
  no operation moved by 1% of the time
where the time goes in v4:
time: 419 us; the launch traced here: 418 us
  Pallas kernels  416 us (99%)
    pallas_call x1, Pallas kernels, local_fn(): pl.pallas_call(functools.partial(encoder_kernel, group, N_CHUNK), out_sha...  416 us

profile of v4, /device:TPU:81, one launch (start us, length us, event | category | flops | bytes accessed | tf_op | source)
XLA Modules:
  0.0 418.4 jit_solution(9579324979894529242)
XLA Ops:
  0.0 416.0 %encoder.1 = bf16[2,64,4672]{2,1,0:T(8,128)(2,1)} custom-call(bf16[2,64,4672]{2,1,0:T(8,128)(2,1)} %tokens.1, s32[2,512]{1,0:T(2,128)} %pad_mask.1, f32[8,32]{1,0:T(8,128)} %bitcast.7, f32[2,4672]{1,0:T(2,128)} %norm_a.1, f32[2,4672]{1,0:T(2,128)} %norm_m.1, bf16[2,4672,512]{2,1,0:T(8,128)(2,1)} %w_query.1, bf16[2,4672,512]{2,1,0:T(8,128)(2,1)} %w_key.1, ...), custom_call_target="tpu_custom_call" | custom-call | tf_op jit(solution)/shard_map/encoder/pallas_call | solution.py:452
  416.0 2.4 copy.14
